TPU v7x, 256 devices: a whole 4x4x8 slice. The times are simulated.
256 devices in a mesh: doc: 8 (over y_lo, x), ctx: 32 (over z, y_hi, core).
Axes of the slice: x: 4, y: 4 (y_hi: 2, y_lo: 2; y = y_hi * 2 + y_lo), z: 8, core: 2. Of those that a mesh axis runs over, the one named last changes fastest.
Arguments:
- queries: bfloat16 [8, 8192, 32, 128], P('doc', 'ctx'), may hold values from -6 to 6
- stored_key_state: bfloat16 [8, 8192, 4, 128], P('doc', 'ctx'), may hold values from -6 to 6
- stored_value_state: bfloat16 [8, 8192, 4, 128], P('doc', 'ctx'), may hold values from -0.5390625 to 0.5390625
- out_grad: bfloat16 [8, 8192, 32, 128], P('doc', 'ctx'), may hold values from -6 to 6
- logsumexp: float32 [8, 32, 8192], P('doc', None, 'ctx'), may hold values from 3 to 5
- row_dots: float32 [8, 32, 8192], P('doc', None, 'ctx'), may hold values from -6 to 6
Outputs:
- query_grad: float32 [8, 8192, 32, 128], P('doc', 'ctx')
- key_grad: float32 [8, 8192, 4, 128], P('doc', 'ctx')
- value_grad: float32 [8, 8192, 4, 128], P('doc', 'ctx')
All inputs are finite; a program needn't handle non-finite values.
Results may differ from a plain program's by a relative error of at most 0.0053.
Values may be sent and summed in bfloat16 or wider, within the bound.
No kernel may reach another device: no remote copies, remote signals or barrier semaphores. Data moves between devices by JAX's collectives and lax.ppermute only.
A program may use at most 64 MiB of HBM per device.

v0:
```python
import jax
import jax.numpy as jnp
from jax import lax
from jax.sharding import PartitionSpec as P


def shifted(x, axis, by):
    count = lax.axis_size(axis)
    pairs = [(i, i + by) for i in range(count) if 0 <= i + by < count]
    return lax.ppermute(x, axis, pairs)


def as_sent(x):

    def short(part):
        return part.astype(jnp.bfloat16) if part.dtype == jnp.float32 else part

    return jax.tree.map(short, x)


def from_behind(value, axis, steps):
    count = lax.axis_size(axis)
    pairs = [(source, (source + steps) % count) for source in range(count)]
    return lax.ppermute(value, axis, pairs)


def score_mask(block_index, length):
    query_pos = lax.broadcasted_iota(jnp.int32, (length, 5 * length), 0)
    key_slot = lax.broadcasted_iota(jnp.int32, (length, 5 * length), 1)
    source = key_slot // length
    within = key_slot % length
    causal = (source == 2) & (within <= query_pos)
    older = ((source == 0) | (source == 3)) & (block_index >= 2)
    recent = ((source == 1) | (source == 4)) & (block_index >= 1)
    return causal | older | recent


def block_backward(query_rows, grad_rows, lse_rows, dot_rows, keys_all, values_all, allowed):
    length, heads, width = query_rows.shape
    groups = keys_all.shape[1]
    per_group = heads // groups
    scaling = width ** (-0.5)
    query_split = query_rows.reshape(length, groups, per_group, width)
    grad_split = grad_rows.reshape(length, groups, per_group, width)
    lse_split = lse_rows.reshape(groups, per_group, length)
    dot_split = dot_rows.reshape(groups, per_group, length)

    def one_group(group_index):
        query_head = lax.dynamic_index_in_dim(query_split, group_index, 1, keepdims=False)
        grad_head = lax.dynamic_index_in_dim(grad_split, group_index, 1, keepdims=False)
        key_head = lax.dynamic_index_in_dim(keys_all, group_index, 1, keepdims=False)
        value_head = lax.dynamic_index_in_dim(values_all, group_index, 1, keepdims=False)
        lse_head = lax.dynamic_index_in_dim(lse_split, group_index, 0, keepdims=False)
        dot_head = lax.dynamic_index_in_dim(dot_split, group_index, 0, keepdims=False)
        scores = (
            jnp.einsum("igd,md->gim", query_head, key_head, preferred_element_type=jnp.float32)
            * scaling
        )
        probs = jnp.where(allowed[None], jnp.exp(scores - lse_head[:, :, None]), jnp.float32(0.0))
        probs_half = probs.astype(jnp.bfloat16)
        value_part = jnp.einsum(
            "gim,igd->md", probs_half, grad_head, preferred_element_type=jnp.float32
        )
        prob_grad = jnp.einsum(
            "igd,md->gim", grad_head, value_head, preferred_element_type=jnp.float32
        )
        score_grad = (probs * (prob_grad - dot_head[:, :, None])).astype(jnp.bfloat16)
        query_part = (
            jnp.einsum("gim,md->igd", score_grad, key_head, preferred_element_type=jnp.float32)
            * scaling
        )
        key_part = (
            jnp.einsum("gim,igd->md", score_grad, query_head, preferred_element_type=jnp.float32)
            * scaling
        )
        return (query_part, key_part, value_part)

    query_part, key_part, value_part = lax.map(one_group, jnp.arange(groups, dtype=jnp.int32))
    query_out = jnp.transpose(query_part, (1, 0, 2, 3)).reshape(length, heads, width)
    return (query_out, jnp.transpose(key_part, (1, 0, 2)), jnp.transpose(value_part, (1, 0, 2)))


def earlier(blocks):
    nearer = shifted(blocks, "ctx", 1)
    farther = shifted(blocks, "ctx", 2)
    return (nearer, farther)


def later(nearer, farther):
    first_back = shifted(as_sent(nearer), "ctx", -1).astype(nearer.dtype)
    return first_back + shifted(as_sent(farther), "ctx", -2).astype(farther.dtype)


def per_device(queries, stored_key_state, stored_value_state, out_grad, logsumexp, row_dots):
    length = queries.shape[1]
    stacked_rows = jnp.stack([stored_key_state[0], stored_value_state[0]])
    nearer, farther = earlier(stacked_rows[None])
    own_near, own_far = (nearer[0], farther[0])
    crossed = from_behind(jnp.stack([own_near, own_far]), "doc", -1)
    part_near, part_far = (crossed[0], crossed[1])
    keys_all = jnp.concatenate(
        [own_far[0], own_near[0], stacked_rows[0], part_far[0], part_near[0]], axis=0
    )
    values_all = jnp.concatenate(
        [own_far[1], own_near[1], stacked_rows[1], part_far[1], part_near[1]], axis=0
    )
    allowed = score_mask(lax.axis_index("ctx"), length)
    query_grad, key_part, value_part = block_backward(
        queries[0], out_grad[0], logsumexp[0], row_dots[0], keys_all, values_all, allowed
    )
    groups = key_part.shape[1]
    width = key_part.shape[2]
    gradients = jnp.stack([key_part, value_part]).reshape(2, 5, length, groups, width)
    returned = from_behind(
        jnp.stack([gradients[:, 4], gradients[:, 3]]).astype(jnp.bfloat16), "doc", 1
    ).astype(jnp.float32)
    arrived = later((gradients[:, 1] + returned[0])[None], (gradients[:, 0] + returned[1])[None])
    reduced_sum = gradients[:, 2] + arrived[0]
    return (query_grad[None], reduced_sum[0][None], reduced_sum[1][None])


def solution(mesh):
    in_specs = (
        P("doc", "ctx", None, None),
        P("doc", "ctx", None, None),
        P("doc", "ctx", None, None),
        P("doc", "ctx", None, None),
        P("doc", None, "ctx"),
        P("doc", None, "ctx"),
    )
    out_specs = (
        P("doc", "ctx", None, None),
        P("doc", "ctx", None, None),
        P("doc", "ctx", None, None),
    )
    return jax.shard_map(
        per_device, mesh=mesh, in_specs=in_specs, out_specs=out_specs, check_vma=False
    )
```

profile of v0, /device:TPU:128, one launch (start us, length us, event | category | flops | bytes accessed | tf_op | source)
XLA Modules:
  0.0 195.3 jit_solution(12933402340548024753)
XLA Ops:
  3.5 1.9 collective-permute-start.1
  5.4 5.1 %collective-permute-start = (bf16[1,2,256,4,128]{4,2,3,1,0:T(8,128)(2,1)}, bf16[1,2,256,4,128]{4,2,3,1,0:T(8,128)(2,1)S(1)}, u32[]{:S(2)}, u32[]{:S(2)}) collective-permute-start(bf16[1,2,256,4,128]{4,2,3,1,0:T(8,128)(2,1)} %maximum_bitcast_fusion), channel_id=1, source_target_pairs={{0,2},{1,3},{2,4},{3,5},{4,6},{5,7},{6,8},{7,9},{8,10},{9,11},{10,... | collective-permute-start | bytes 1572872 | tf_op jit(solution)/shard_map/ppermute | solution.py:10
  10.5 2.4 %copy.14 = bf16[1,256,32,128]{3,1,2,0:T(8,128)(2,1)S(1)} copy(bf16[1,256,32,128]{3,2,1,0:T(8,128)(2,1)} %param.8) | data formatting | bytes 4194304 | tf_op args[0]
  12.9 3.8 %copy.16 = bf16[1,256,32,128]{3,1,2,0:T(8,128)(2,1)} copy(bf16[1,256,32,128]{3,2,1,0:T(8,128)(2,1)} %param.11) | data formatting | bytes 4194304 | tf_op args[3]
  16.7 4.2 %collective-permute-done.1 = bf16[1,2,256,4,128]{4,2,3,1,0:T(8,128)(2,1)S(1)} collective-permute-done((bf16[1,2,256,4,128]{4,2,3,1,0:T(8,128)(2,1)}, bf16[1,2,256,4,128]{4,2,3,1,0:T(8,128)(2,1)S(1)}, u32[]{:S(2)}, u32[]{:S(2)}) %collective-permute-start.1) | collective-permute-done | bytes 524320 | tf_op jit(solution)/shard_map/ppermute | solution.py:10
  20.9 5.0 %collective-permute-done = bf16[1,2,256,4,128]{4,2,3,1,0:T(8,128)(2,1)S(1)} collective-permute-done((bf16[1,2,256,4,128]{4,2,3,1,0:T(8,128)(2,1)}, bf16[1,2,256,4,128]{4,2,3,1,0:T(8,128)(2,1)S(1)}, u32[]{:S(2)}, u32[]{:S(2)}) %collective-permute-start) | collective-permute-done | bytes 524320 | tf_op jit(solution)/shard_map/ppermute | solution.py:10
  26.0 4.0 %collective-permute-start.2 = (bf16[2,2,256,4,128]{4,2,3,1,0:T(8,128)(2,1)S(1)}, bf16[2,2,256,4,128]{4,2,3,1,0:T(8,128)(2,1)S(1)}, u32[]{:S(2)}, u32[]{:S(2)}) collective-permute-start(bf16[2,2,256,4,128]{4,2,3,1,0:T(8,128)(2,1)S(1)} %pad_maximum_fusion.1), channel_id=1, source_target_pairs={{0,224},{32,0},{64,32},{96,64},{128,96},{160,128},{192,160},{224,1... | collective-permute-start | bytes 3145736 | tf_op jit(solution)/shard_map/ppermute | solution.py:24
  32.4 19.2 %collective-permute-done.2 = bf16[2,2,256,4,128]{4,2,3,1,0:T(8,128)(2,1)S(1)} collective-permute-done((bf16[2,2,256,4,128]{4,2,3,1,0:T(8,128)(2,1)S(1)}, bf16[2,2,256,4,128]{4,2,3,1,0:T(8,128)(2,1)S(1)}, u32[]{:S(2)}, u32[]{:S(2)}) %collective-permute-start.2) | collective-permute-done | bytes 1048608 | tf_op jit(solution)/shard_map/ppermute | solution.py:24
  52.8 71.3 %while.15 = (s32[]{:T(128)}, f32[4,256,8,128]{1,3,2,0:T(8,128)}, f32[4,1280,128]{2,1,0:T(8,128)}, f32[4,1280,128]{2,1,0:T(8,128)}, s32[4]{0:T(128)S(1)}, /*index...) while((s32[]{:T(128)}, f32[4,256,8,128]{1,3,2,0:T(8,128)}, ...), condition=%wide.region_1.2_spmd.clone, body=%wide.region_0.1_spmd.clone.sunk | while | flops 3386998784 | bytes 62079796 | solution.py:78
  59.3 2.8 %fusion.110 = f32[4,1280,128]{2,1,0:T(8,128)} fusion(f32[4,1280,128]{2,1,0:T(8,128)} %get-tuple-element.324, s32[]{:T(128)S(6)} %copy.40, f32[1280,256,8]{1,0,2:T(8,128)S(1)} %fusion.105, f32[8,256]{1,0:T(8,128)S(1)} %get-tuple-element.298, pred[256,1280]{0,1:T(8,128)(4,1)S(1)} %fusion.106, bf16[256,4,8,128]{3,0,2,1:T(8,128)(2,1)S(1)} %copy-done.2, ...), kind=kOutput, calls=%fused_computation.16.clone.1 | convolution fusion | flops 681574400 | bytes 12001288 | tf_op jit(solution)/shard_map/while/body/eval_jaxpr/gim,igd->md/dot_general | solution.py:61
  62.0 4.3 %fusion.107 = bf16[8,256,1280]{1,2,0:T(8,128)(2,1)S(1)} fusion(f32[1280,256,8]{1,0,2:T(8,128)S(1)} %fusion.105, f32[8,256]{1,0:T(8,128)S(1)} %get-tuple-element.297, f32[8,256]{1,0:T(8,128)S(1)} %get-tuple-element.298, pred[256,1280]{0,1:T(8,128)(4,1)S(1)} %fusion.106, bf16[256,4,8,128]{3,0,2,1:T(8,128)(2,1)S(1)} %copy-done.2, s32[]{:T(128)S(6)} %select_n.108, ...), kind=kOutput, calls=%fused_computation.3.clone.1 | convolution fusion | flops 686817280 | bytes 16925696 | tf_op jit(solution)/shard_map/while/body/eval_jaxpr/igd,md->gim/dot_general | solution.py:64
  66.4 2.4 %fusion.109 = f32[4,1280,128]{2,1,0:T(8,128)} fusion(f32[4,1280,128]{2,1,0:T(8,128)} %get-tuple-element.323, s32[]{:T(128)S(6)} %copy.40, bf16[8,256,1280]{1,2,0:T(8,128)(2,1)S(1)} %fusion.107, bf16[256,4,8,128]{3,0,2,1:T(8,128)(2,1)S(1)} %get-tuple-element.349, s32[]{:T(128)S(6)} %select_n.108), kind=kOutput, calls=%fused_computation.20.clone.1 | convolution fusion | flops 671252480 | bytes 6422536 | tf_op jit(solution)/shard_map/while/body/eval_jaxpr/gim,igd->md/dot_general | solution.py:73
  68.7 1.9 fusion.108
  77.1 2.8 %fusion.110 = f32[4,1280,128]{2,1,0:T(8,128)} fusion(f32[4,1280,128]{2,1,0:T(8,128)} %get-tuple-element.324, s32[]{:T(128)S(6)} %copy.40, f32[1280,256,8]{1,0,2:T(8,128)S(1)} %fusion.105, f32[8,256]{1,0:T(8,128)S(1)} %get-tuple-element.298, pred[256,1280]{0,1:T(8,128)(4,1)S(1)} %fusion.106, bf16[256,4,8,128]{3,0,2,1:T(8,128)(2,1)S(1)} %copy-done.2, ...), kind=kOutput, calls=%fused_computation.16.clone.1 | convolution fusion | flops 681574400 | bytes 12001288 | tf_op jit(solution)/shard_map/while/body/eval_jaxpr/gim,igd->md/dot_general | solution.py:61
  79.9 4.3 %fusion.107 = bf16[8,256,1280]{1,2,0:T(8,128)(2,1)S(1)} fusion(f32[1280,256,8]{1,0,2:T(8,128)S(1)} %fusion.105, f32[8,256]{1,0:T(8,128)S(1)} %get-tuple-element.297, f32[8,256]{1,0:T(8,128)S(1)} %get-tuple-element.298, pred[256,1280]{0,1:T(8,128)(4,1)S(1)} %fusion.106, bf16[256,4,8,128]{3,0,2,1:T(8,128)(2,1)S(1)} %copy-done.2, s32[]{:T(128)S(6)} %select_n.108, ...), kind=kOutput, calls=%fused_computation.3.clone.1 | convolution fusion | flops 686817280 | bytes 16925696 | tf_op jit(solution)/shard_map/while/body/eval_jaxpr/igd,md->gim/dot_general | solution.py:64
  84.3 2.4 %fusion.109 = f32[4,1280,128]{2,1,0:T(8,128)} fusion(f32[4,1280,128]{2,1,0:T(8,128)} %get-tuple-element.323, s32[]{:T(128)S(6)} %copy.40, bf16[8,256,1280]{1,2,0:T(8,128)(2,1)S(1)} %fusion.107, bf16[256,4,8,128]{3,0,2,1:T(8,128)(2,1)S(1)} %get-tuple-element.349, s32[]{:T(128)S(6)} %select_n.108), kind=kOutput, calls=%fused_computation.20.clone.1 | convolution fusion | flops 671252480 | bytes 6422536 | tf_op jit(solution)/shard_map/while/body/eval_jaxpr/gim,igd->md/dot_general | solution.py:73
  86.6 1.9 fusion.108
  94.9 2.8 %fusion.110 = f32[4,1280,128]{2,1,0:T(8,128)} fusion(f32[4,1280,128]{2,1,0:T(8,128)} %get-tuple-element.324, s32[]{:T(128)S(6)} %copy.40, f32[1280,256,8]{1,0,2:T(8,128)S(1)} %fusion.105, f32[8,256]{1,0:T(8,128)S(1)} %get-tuple-element.298, pred[256,1280]{0,1:T(8,128)(4,1)S(1)} %fusion.106, bf16[256,4,8,128]{3,0,2,1:T(8,128)(2,1)S(1)} %copy-done.2, ...), kind=kOutput, calls=%fused_computation.16.clone.1 | convolution fusion | flops 681574400 | bytes 12001288 | tf_op jit(solution)/shard_map/while/body/eval_jaxpr/gim,igd->md/dot_general | solution.py:61
  97.7 4.3 %fusion.107 = bf16[8,256,1280]{1,2,0:T(8,128)(2,1)S(1)} fusion(f32[1280,256,8]{1,0,2:T(8,128)S(1)} %fusion.105, f32[8,256]{1,0:T(8,128)S(1)} %get-tuple-element.297, f32[8,256]{1,0:T(8,128)S(1)} %get-tuple-element.298, pred[256,1280]{0,1:T(8,128)(4,1)S(1)} %fusion.106, bf16[256,4,8,128]{3,0,2,1:T(8,128)(2,1)S(1)} %copy-done.2, s32[]{:T(128)S(6)} %select_n.108, ...), kind=kOutput, calls=%fused_computation.3.clone.1 | convolution fusion | flops 686817280 | bytes 16925696 | tf_op jit(solution)/shard_map/while/body/eval_jaxpr/igd,md->gim/dot_general | solution.py:64
  102.1 2.4 %fusion.109 = f32[4,1280,128]{2,1,0:T(8,128)} fusion(f32[4,1280,128]{2,1,0:T(8,128)} %get-tuple-element.323, s32[]{:T(128)S(6)} %copy.40, bf16[8,256,1280]{1,2,0:T(8,128)(2,1)S(1)} %fusion.107, bf16[256,4,8,128]{3,0,2,1:T(8,128)(2,1)S(1)} %get-tuple-element.349, s32[]{:T(128)S(6)} %select_n.108), kind=kOutput, calls=%fused_computation.20.clone.1 | convolution fusion | flops 671252480 | bytes 6422536 | tf_op jit(solution)/shard_map/while/body/eval_jaxpr/gim,igd->md/dot_general | solution.py:73
  104.4 1.9 fusion.108
  112.8 2.8 %fusion.110 = f32[4,1280,128]{2,1,0:T(8,128)} fusion(f32[4,1280,128]{2,1,0:T(8,128)} %get-tuple-element.324, s32[]{:T(128)S(6)} %copy.40, f32[1280,256,8]{1,0,2:T(8,128)S(1)} %fusion.105, f32[8,256]{1,0:T(8,128)S(1)} %get-tuple-element.298, pred[256,1280]{0,1:T(8,128)(4,1)S(1)} %fusion.106, bf16[256,4,8,128]{3,0,2,1:T(8,128)(2,1)S(1)} %copy-done.2, ...), kind=kOutput, calls=%fused_computation.16.clone.1 | convolution fusion | flops 681574400 | bytes 12001288 | tf_op jit(solution)/shard_map/while/body/eval_jaxpr/gim,igd->md/dot_general | solution.py:61
  115.6 4.3 %fusion.107 = bf16[8,256,1280]{1,2,0:T(8,128)(2,1)S(1)} fusion(f32[1280,256,8]{1,0,2:T(8,128)S(1)} %fusion.105, f32[8,256]{1,0:T(8,128)S(1)} %get-tuple-element.297, f32[8,256]{1,0:T(8,128)S(1)} %get-tuple-element.298, pred[256,1280]{0,1:T(8,128)(4,1)S(1)} %fusion.106, bf16[256,4,8,128]{3,0,2,1:T(8,128)(2,1)S(1)} %copy-done.2, s32[]{:T(128)S(6)} %select_n.108, ...), kind=kOutput, calls=%fused_computation.3.clone.1 | convolution fusion | flops 686817280 | bytes 16925696 | tf_op jit(solution)/shard_map/while/body/eval_jaxpr/igd,md->gim/dot_general | solution.py:64
  119.9 2.4 %fusion.109 = f32[4,1280,128]{2,1,0:T(8,128)} fusion(f32[4,1280,128]{2,1,0:T(8,128)} %get-tuple-element.323, s32[]{:T(128)S(6)} %copy.40, bf16[8,256,1280]{1,2,0:T(8,128)(2,1)S(1)} %fusion.107, bf16[256,4,8,128]{3,0,2,1:T(8,128)(2,1)S(1)} %get-tuple-element.349, s32[]{:T(128)S(6)} %select_n.108), kind=kOutput, calls=%fused_computation.20.clone.1 | convolution fusion | flops 671252480 | bytes 6422536 | tf_op jit(solution)/shard_map/while/body/eval_jaxpr/gim,igd->md/dot_general | solution.py:73
  124.1 6.2 %copy.19 = f32[1280,4,128]{2,1,0:T(4,128)S(1)} copy(f32[1280,4,128]{2,0,1:T(8,128)} %bitcast.188) | data formatting | bytes 5242880 | tf_op jit(solution)/shard_map/transpose | solution.py:80
  130.4 5.7 %copy.18 = f32[1280,4,128]{2,1,0:T(4,128)S(1)} copy(f32[1280,4,128]{2,0,1:T(8,128)S(1)} %bitcast.189) | data formatting | bytes 5242880 | tf_op jit(solution)/shard_map/transpose | solution.py:80
  138.9 27.3 %collective-permute-done.3 = bf16[2,2,256,4,128]{4,3,2,1,0:T(4,128)(2,1)S(1)} collective-permute-done((bf16[2,2,256,4,128]{4,3,2,1,0:T(4,128)(2,1)S(1)}, bf16[2,2,256,4,128]{4,3,2,1,0:T(4,128)(2,1)S(1)}, u32[]{:S(2)}, u32[]{:S(2)}) %collective-permute-start.3) | collective-permute-done | bytes 1048608 | tf_op jit(solution)/shard_map/ppermute | solution.py:24
  168.0 2.5 %collective-permute-start.4 = (bf16[1,2,256,4,128]{4,3,2,1,0:T(4,128)(2,1)}, bf16[1,2,256,4,128]{4,3,2,1,0:T(4,128)(2,1)S(1)}, u32[]{:S(2)}, u32[]{:S(2)}) collective-permute-start(bf16[1,2,256,4,128]{4,3,2,1,0:T(4,128)(2,1)} %get-tuple-element.158), channel_id=1, source_target_pairs={{1,0},{2,1},{3,2},{4,3},{5,4},{6,5},{7,6},{8,7},{9,8},{10,9},{11,1... | collective-permute-start | bytes 1572872 | tf_op jit(solution)/shard_map/ppermute | solution.py:10
  170.5 3.7 %collective-permute-start.5 = (bf16[1,2,256,4,128]{4,3,2,1,0:T(4,128)(2,1)}, bf16[1,2,256,4,128]{4,3,2,1,0:T(4,128)(2,1)}, u32[]{:S(2)}, u32[]{:S(2)}) collective-permute-start(bf16[1,2,256,4,128]{4,3,2,1,0:T(4,128)(2,1)} %get-tuple-element.159), channel_id=1, source_target_pairs={{2,0},{3,1},{4,2},{5,3},{6,4},{7,5},{8,6},{9,7},{10,8},{11,9},{12,... | collective-permute-start | bytes 1572872 | tf_op jit(solution)/shard_map/ppermute | solution.py:10
  174.2 5.4 %copy.17 = f32[256,4,8,128]{3,2,1,0:T(8,128)} copy(f32[256,4,8,128]{0,3,2,1:T(8,128)} %bitcast.186) | data formatting | bytes 8388608 | tf_op jit(solution)/shard_map/transpose | solution.py:79
  179.6 2.0 %collective-permute-done.4 = bf16[1,2,256,4,128]{4,3,2,1,0:T(4,128)(2,1)S(1)} collective-permute-done((bf16[1,2,256,4,128]{4,3,2,1,0:T(4,128)(2,1)}, bf16[1,2,256,4,128]{4,3,2,1,0:T(4,128)(2,1)S(1)}, u32[]{:S(2)}, u32[]{:S(2)}) %collective-permute-start.4) | collective-permute-done | bytes 524320 | tf_op jit(solution)/shard_map/ppermute | solution.py:10
  181.6 11.0 %collective-permute-done.5 = bf16[1,2,256,4,128]{4,3,2,1,0:T(4,128)(2,1)} collective-permute-done((bf16[1,2,256,4,128]{4,3,2,1,0:T(4,128)(2,1)}, bf16[1,2,256,4,128]{4,3,2,1,0:T(4,128)(2,1)}, u32[]{:S(2)}, u32[]{:S(2)}) %collective-permute-start.5) | collective-permute-done | bytes 524320 | tf_op jit(solution)/shard_map/ppermute | solution.py:10
  (63 shorter events, 33.6 us)
Async XLA Ops:
  3.5 17.4 %collective-permute-start.1 = (bf16[1,2,256,4,128]{4,2,3,1,0:T(8,128)(2,1)}, bf16[1,2,256,4,128]{4,2,3,1,0:T(8,128)(2,1)S(1)}, u32[]{:S(2)}, u32[]{:S(2)}) collective-permute-start(bf16[1,2,256,4,128]{4,2,3,1,0:T(8,128)(2,1)} %maximum_bitcast_fusion), channel_id=1, source_target_pairs={{0,1},{1,2},{2,3},{3,4},{4,5},{5,6},{6,7},{7,8},{8,9},{9,10},{10,1... | collective-permute-start | bytes 1572872 | tf_op jit(solution)/shard_map/ppermute | solution.py:10
  5.4 20.5 %collective-permute-start = (bf16[1,2,256,4,128]{4,2,3,1,0:T(8,128)(2,1)}, bf16[1,2,256,4,128]{4,2,3,1,0:T(8,128)(2,1)S(1)}, u32[]{:S(2)}, u32[]{:S(2)}) collective-permute-start(bf16[1,2,256,4,128]{4,2,3,1,0:T(8,128)(2,1)} %maximum_bitcast_fusion), channel_id=1, source_target_pairs={{0,2},{1,3},{2,4},{3,5},{4,6},{5,7},{6,8},{7,9},{8,10},{9,11},{10,... | collective-permute-start | bytes 1572872 | tf_op jit(solution)/shard_map/ppermute | solution.py:10
  16.7 15.5 %copy-start.5 = (bf16[1,256,4,128]{3,2,1,0:T(4,128)(2,1)S(1)}, bf16[1,256,4,128]{3,2,1,0:T(4,128)(2,1)}, u32[]{:S(2)}) copy-start(bf16[1,256,4,128]{3,2,1,0:T(4,128)(2,1)} %param.10) | copy-start | bytes 786436
  16.7 15.6 %copy-start.6 = (bf16[1,256,4,128]{3,2,1,0:T(4,128)(2,1)S(1)}, bf16[1,256,4,128]{3,2,1,0:T(4,128)(2,1)}, u32[]{:S(2)}) copy-start(bf16[1,256,4,128]{3,2,1,0:T(4,128)(2,1)} %param.9) | copy-start | bytes 786436
  20.9 9.2 %copy-start.3 = (bf16[1,2,256,4,128]{4,2,3,1,0:T(8,128)(2,1)}, bf16[1,2,256,4,128]{4,2,3,1,0:T(8,128)(2,1)S(1)}, u32[]{:S(2)}) copy-start(bf16[1,2,256,4,128]{4,2,3,1,0:T(8,128)(2,1)S(1)} %collective-permute-done.1) | copy-start | bytes 1572868
  25.9 4.2 %copy-start.4 = (bf16[1,2,256,4,128]{4,2,3,1,0:T(8,128)(2,1)}, bf16[1,2,256,4,128]{4,2,3,1,0:T(8,128)(2,1)S(1)}, u32[]{:S(2)}) copy-start(bf16[1,2,256,4,128]{4,2,3,1,0:T(8,128)(2,1)S(1)} %collective-permute-done) | copy-start | bytes 1572868
  26.0 25.6 %collective-permute-start.2 = (bf16[2,2,256,4,128]{4,2,3,1,0:T(8,128)(2,1)S(1)}, bf16[2,2,256,4,128]{4,2,3,1,0:T(8,128)(2,1)S(1)}, u32[]{:S(2)}, u32[]{:S(2)}) collective-permute-start(bf16[2,2,256,4,128]{4,2,3,1,0:T(8,128)(2,1)S(1)} %pad_maximum_fusion.1), channel_id=1, source_target_pairs={{0,224},{32,0},{64,32},{96,64},{128,96},{160,128},{192,160},{224,1... | collective-permute-start | bytes 3145736 | tf_op jit(solution)/shard_map/ppermute | solution.py:24
  51.8 1.0 copy-start.7
  57.7 1.6 copy-start.2
  75.5 1.6 copy-start.2
  93.4 1.6 copy-start.2
  111.2 1.6 copy-start.2
  124.1 6.2 %copy-start.1 = (f32[4,1280,128]{2,1,0:T(8,128)S(1)}, f32[4,1280,128]{2,1,0:T(8,128)}, u32[]{:S(2)}) copy-start(f32[4,1280,128]{2,1,0:T(8,128)} %get-tuple-element.68) | copy-start | bytes 7864324
  136.0 30.3 %copy-start = (f32[1280,4,128]{2,1,0:T(4,128)}, f32[1280,4,128]{2,1,0:T(4,128)S(1)}, u32[]{:S(2)}) copy-start(f32[1280,4,128]{2,1,0:T(4,128)S(1)} %copy.18) | copy-start | bytes 7864324
  138.6 27.6 %collective-permute-start.3 = (bf16[2,2,256,4,128]{4,3,2,1,0:T(4,128)(2,1)S(1)}, bf16[2,2,256,4,128]{4,3,2,1,0:T(4,128)(2,1)S(1)}, u32[]{:S(2)}, u32[]{:S(2)}) collective-permute-start(bf16[2,2,256,4,128]{4,3,2,1,0:T(4,128)(2,1)S(1)} %pad_maximum_fusion.2), channel_id=1, source_target_pairs={{0,32},{32,64},{64,96},{96,128},{128,160},{160,192},{192,224},{224... | collective-permute-start | bytes 3145736 | tf_op jit(solution)/shard_map/ppermute | solution.py:24
  168.0 13.6 %collective-permute-start.4 = (bf16[1,2,256,4,128]{4,3,2,1,0:T(4,128)(2,1)}, bf16[1,2,256,4,128]{4,3,2,1,0:T(4,128)(2,1)S(1)}, u32[]{:S(2)}, u32[]{:S(2)}) collective-permute-start(bf16[1,2,256,4,128]{4,3,2,1,0:T(4,128)(2,1)} %get-tuple-element.158), channel_id=1, source_target_pairs={{1,0},{2,1},{3,2},{4,3},{5,4},{6,5},{7,6},{8,7},{9,8},{10,9},{11,1... | collective-permute-start | bytes 1572872 | tf_op jit(solution)/shard_map/ppermute | solution.py:10
  170.5 22.1 %collective-permute-start.5 = (bf16[1,2,256,4,128]{4,3,2,1,0:T(4,128)(2,1)}, bf16[1,2,256,4,128]{4,3,2,1,0:T(4,128)(2,1)}, u32[]{:S(2)}, u32[]{:S(2)}) collective-permute-start(bf16[1,2,256,4,128]{4,3,2,1,0:T(4,128)(2,1)} %get-tuple-element.159), channel_id=1, source_target_pairs={{2,0},{3,1},{4,2},{5,3},{6,4},{7,5},{8,6},{9,7},{10,8},{11,9},{12,... | collective-permute-start | bytes 1572872 | tf_op jit(solution)/shard_map/ppermute | solution.py:10
where the time goes:
time: 196 us; the launch traced here: 195 us
  waiting for transfers between devices  68.7 us (35%)
  matrix products  51.5 us (26%)
  local copies, waits for them, and re-layouts  35.8 us (18%)
  starting transfers between devices  17.5 us (9%)
  other arithmetic  13.1 us (7%)
  loops' own time  7.9 us (4%)
    ppermute x2, waiting for transfers between devices, from_behind(): return lax.ppermute(value, axis, pairs)  46.5 us
    ppermute x4, waiting for transfers between devices, shifted(): return lax.ppermute(x, axis, pairs)  22.2 us
    dot_general x4, matrix products, one_group(): jnp.einsum('igd,md->gim', grad_head, value_head, preferred_element_type=j...  17.3 us
    ppermute x4, starting transfers between devices, shifted(): return lax.ppermute(x, axis, pairs)  13.2 us
    unnamed x22, local copies, waits for them, and re-layouts  11.6 us
    dot_general x4, matrix products, one_group(): jnp.einsum('gim,igd->md', probs_half, grad_head, preferred_element_type=j...  11.1 us
    dot_general x4, matrix products, one_group(): jnp.einsum('gim,igd->md', score_grad, query_head, preferred_element_type=...  9.47 us
    another operation x1, loops' own time, block_backward(): lax.map(one_group, jnp.arange(groups, dtype=jnp.int32))  7.9 us
  transfers between devices with their start and end apart: 6, of which 6 were waited for; matrix products, arithmetic and copies ran while one was open for 7% of the time, Pallas kernels for 0%

commit v1 on v0

v1 whole, which is shorter than its diff:
```python
import functools
import math

import jax
import jax.numpy as jnp
from jax import lax
from jax.experimental import pallas as pl
from jax.experimental.pallas import tpu as pltpu
from jax.sharding import PartitionSpec as P

LOG2E = math.log2(math.e)
F32, BF16 = jnp.float32, jnp.bfloat16
NT = (((1,), (1,)), ((), ()))
NN = (((1,), (0,)), ((), ()))
TN = (((0,), (0,)), ((), ()))


def mm(a, b, dims):
    return lax.dot_general(a, b, dims, preferred_element_type=F32)


def columns(width, q, g, lse_ref, dot_ref, sl, k, v, mask):
    qc, gc = q[sl, :], g[sl, :]
    s = mm(k, qc, NT)
    p = jnp.exp2(s * (LOG2E * width**-0.5) - lse_ref[0, :, sl])
    if mask is not None:
        p = jnp.where(mask, p, 0.0)
    dv = mm(p.astype(BF16), gc, NN)
    dp = mm(v, gc, NT)
    ds = (p * (dp - dot_ref[0, :, sl])).astype(BF16)
    dk = mm(ds, qc, NN)
    dq = mm(ds, k, TN)
    return dq, dk, dv


def pair_kernel(cw, n_near, first, q_ref, g_ref, lse_ref, dot_ref, far_ref, *rest):
    near_refs, rest = rest[:n_near], rest[n_near:]
    prev_ref = None
    if not first:
        prev_ref, *rest = rest
    dq_ref, near_out, far_out = rest
    tokens, heads, width = q_ref.shape
    n = tokens * heads
    q, g = q_ref.reshape(n, width), g_ref.reshape(n, width)
    near_k, near_v = near_refs[0][0, 0], near_refs[0][1, 0]
    for other in near_refs[1:]:
        near_k, near_v = near_k + other[0, 0], near_v + other[1, 0]
    k = jnp.concatenate([far_ref[0, 0], near_k], axis=0)
    v = jnp.concatenate([far_ref[1, 0], near_v], axis=0)
    dk = dv = None
    for c in range(n // cw):
        sl = pl.ds(c * cw, cw)
        dqc, dkc, dvc = columns(width, q, g, lse_ref, dot_ref, sl, k, v, None)
        if prev_ref is not None:
            dqc = dqc + prev_ref.reshape(n, width)[sl, :]
        dq_ref.reshape(n, width)[sl, :] = dqc
        dk = dkc if dk is None else dk + dkc
        dv = dvc if dv is None else dv + dvc
    dk = dk * width**-0.5
    far_out[0, 0] = dk[:tokens]
    far_out[1, 0] = dv[:tokens]
    near_out[0, 0] = dk[tokens:].astype(BF16)
    near_out[1, 0] = dv[tokens:].astype(BF16)


def own_kernel(cw, q_ref, g_ref, lse_ref, dot_ref, kv_ref, prev_ref, dq_ref, own_out):
    tokens, heads, width = q_ref.shape
    n = tokens * heads
    q, g = q_ref.reshape(n, width), g_ref.reshape(n, width)
    own_out[...] = jnp.zeros_like(own_out)
    for c in range(n // cw):
        sl = pl.ds(c * cw, cw)
        seen = (c + 1) * cw // heads
        k, v = kv_ref[0, 0, :seen, :], kv_ref[1, 0, :seen, :]
        key = lax.broadcasted_iota(jnp.int32, (seen, cw), 0)
        column = lax.broadcasted_iota(jnp.int32, (seen, cw), 1) + c * cw
        dqc, dkc, dvc = columns(width, q, g, lse_ref, dot_ref, sl, k, v, key * heads <= column)
        dqc = dqc + prev_ref.reshape(n, width)[sl, :]
        dq_ref.reshape(n, width)[sl, :] = dqc * width**-0.5
        own_out[0, 0, :seen, :] += dkc * width**-0.5
        own_out[1, 0, :seen, :] += dvc


def specs(tokens, heads, groups, width):
    per = heads // groups
    row = pl.BlockSpec((tokens, per, width), lambda j: (0, j, 0))
    vec = pl.BlockSpec((1, 1, tokens * per), lambda j: (j, 0, 0))
    blk = pl.BlockSpec((2, 1, tokens, width), lambda j: (0, j, 0, 0))
    return row, vec, blk


def pair_call(name, q, g, lse, dots, far, nears, prev):
    tokens, heads, width = q.shape
    groups = far.shape[1]
    row, vec, blk = specs(tokens, heads, groups, width)
    pairs = 2 * tokens * heads * tokens
    args = [q, g, lse, dots, far, *nears] + ([] if prev is None else [prev])
    return pl.pallas_call(
        functools.partial(pair_kernel, 512, len(nears), prev is None),
        grid=(groups,),
        in_specs=[row, row, vec, vec, blk] + [blk] * len(nears) + ([] if prev is None else [row]),
        out_specs=[row, blk, blk],
        out_shape=[
            jax.ShapeDtypeStruct(q.shape, F32),
            jax.ShapeDtypeStruct(far.shape, BF16),
            jax.ShapeDtypeStruct(far.shape, F32),
        ],
        compiler_params=pltpu.CompilerParams(dimension_semantics=("arbitrary",)),
        cost_estimate=pl.CostEstimate(
            flops=10 * pairs * width, transcendentals=pairs, bytes_accessed=16 << 20
        ),
        name=name,
    )(*args)


def own_call(q, g, lse, dots, kv, prev):
    tokens, heads, width = q.shape
    groups = kv.shape[1]
    row, vec, blk = specs(tokens, heads, groups, width)
    pairs = tokens * heads * tokens
    return pl.pallas_call(
        functools.partial(own_kernel, 512),
        grid=(groups,),
        in_specs=[row, row, vec, vec, blk, row],
        out_specs=[row, blk],
        out_shape=[jax.ShapeDtypeStruct(q.shape, F32), jax.ShapeDtypeStruct(kv.shape, F32)],
        compiler_params=pltpu.CompilerParams(dimension_semantics=("arbitrary",)),
        cost_estimate=pl.CostEstimate(
            flops=10 * pairs * width, transcendentals=pairs, bytes_accessed=16 << 20
        ),
        name="own",
    )(q, g, lse, dots, kv, prev)


def send(x, by_doc, to):
    docs, ctxs = lax.axis_size("doc"), lax.axis_size("ctx")
    pairs = []
    for d in range(docs):
        for c in range(ctxs):
            t = to(c)
            if t is not None and 0 <= t < ctxs:
                pairs.append((d * ctxs + c, (d + by_doc) % docs * ctxs + t))
    return lax.ppermute(x, ("doc", "ctx"), pairs)


def ahead(c):
    return c + 2


def back(c):
    return c - 2


def swap(c):
    return c ^ 1


def even_to_odd(c):
    return c + 1 if c % 2 == 0 else None


def odd_to_even(c):
    return c - 1 if c % 2 == 1 else None


def by_group(x, groups):
    heads, tokens = x.shape
    return x.reshape(groups, heads // groups, tokens).transpose(0, 2, 1).reshape(groups, 1, -1)


def per_device(queries, stored_key_state, stored_value_state, out_grad, logsumexp, row_dots):
    groups = stored_key_state.shape[2]
    q, g = queries[0], out_grad[0]
    odd = lax.axis_index("ctx") % 2 == 1
    kv = jnp.stack([stored_key_state[0], stored_value_state[0]]).transpose(0, 2, 1, 3)

    part_far = send(kv, -1, ahead)
    part_near_odd = send(kv, -1, even_to_odd)
    part_near_even = send(part_far, 0, odd_to_even)
    kv_later, _ = lax.optimization_barrier((kv, part_far))
    own_far = send(kv_later, 0, ahead)
    own_near = send(jnp.where(odd, own_far, kv), 0, swap)

    lse = by_group(logsumexp[0] * LOG2E, groups)
    dots = by_group(row_dots[0], groups)

    dq, part_near_grad, part_far_grad = pair_call(
        "partner", q, g, lse, dots, part_far, [part_near_odd, part_near_even], None
    )
    near_home = send(part_near_grad, 1, odd_to_even)
    near_mate = send(part_near_grad, 0, even_to_odd)
    part_home = send((part_far_grad + near_mate.astype(F32)).astype(BF16), 1, back)

    dq, own_near_grad, own_far_grad = pair_call(
        "earlier", q, g, lse, dots, own_far, [own_near], dq
    )
    swapped = send(own_near_grad, 0, swap).astype(F32)
    own_home = send((own_far_grad + jnp.where(odd, swapped, 0.0)).astype(BF16), 0, back)

    dq, own_grad = own_call(q, g, lse, dots, kv, dq)
    total = own_grad + jnp.where(odd, 0.0, swapped) + near_home.astype(F32)
    total = total + part_home.astype(F32) + own_home.astype(F32)
    total = total.transpose(0, 2, 1, 3)
    return dq[None], total[0][None], total[1][None]


def solution(mesh):
    rows, vecs = P("doc", "ctx", None, None), P("doc", None, "ctx")
    return jax.shard_map(
        per_device,
        mesh=mesh,
        in_specs=(rows, rows, rows, rows, vecs, vecs),
        out_specs=(rows, rows, rows),
        check_vma=False,
    )
```

time: 196 us -> 120 us (0.61)
  the two profiles are of different devices: /device:TPU:128 before, /device:TPU:121 now
where the time goes in v1:
time: 120 us
  Pallas kernels  40.3 us (34%)
  starting transfers between devices  35.3 us (29%)
  waiting for transfers between devices  32.1 us (27%)
  local copies, waits for them, and re-layouts  7.3 us (6%)
  other arithmetic  3.9 us (3%)
    ppermute x10, starting transfers between devices, send(): return lax.ppermute(x, ('doc', 'ctx'), pairs)  35.3 us
    ppermute x10, waiting for transfers between devices, send(): return lax.ppermute(x, ('doc', 'ctx'), pairs)  32.1 us
    pallas_call x2, Pallas kernels, pair_call(): pl.pallas_call(functools.partial(pair_kernel, 512, len(nears), prev is No...  29.7 us
    pallas_call x1, Pallas kernels, own_call(): pl.pallas_call(functools.partial(own_kernel, 512), grid=(groups,), in_spe...  10.6 us
    unnamed x16, local copies, waits for them, and re-layouts  5.05 us
  transfers between devices with their start and end apart: 10, of which 4 were waited for; matrix products, arithmetic and copies ran while one was open for 4% of the time, Pallas kernels for 34%

profile of v1, /device:TPU:121, one launch (start us, length us, event | category | flops | bytes accessed | tf_op | source)
XLA Modules:
  0.0 119.8 jit_solution(14634305484459662055)
XLA Ops:
  0.6 1.0 copy.17
  1.6 1.0 copy.18
  2.7 6.6 %collective-permute-start = (bf16[2,4,256,128]{3,2,1,0:T(8,128)(2,1)S(1)}, bf16[2,4,256,128]{3,2,1,0:T(8,128)(2,1)S(1)}, u32[]{:S(2)}, u32[]{:S(2)}) collective-permute-start(bf16[2,4,256,128]{3,2,1,0:T(8,128)(2,1)S(1)} %maximum_bitcast_fusion.kv_ref), channel_id=1, source_target_pairs={{0,226},{1,227},{2,228},{3,229},{4,230},{5,231},{6,232},{7,233},{8... | collective-permute-start | bytes 1572872 | tf_op jit(solution)/shard_map/ppermute | solution.py:143
  9.3 10.6 %collective-permute-done.far_ref = bf16[2,4,256,128]{3,2,1,0:T(8,128)(2,1)S(1)} collective-permute-done((bf16[2,4,256,128]{3,2,1,0:T(8,128)(2,1)S(1)}, bf16[2,4,256,128]{3,2,1,0:T(8,128)(2,1)S(1)}, u32[]{:S(2)}, u32[]{:S(2)}) %collective-permute-start) | collective-permute-done | bytes 524320 | tf_op jit(solution)/shard_map/ppermute | solution.py:143
  19.9 7.4 %collective-permute-start.1 = (bf16[2,4,256,128]{3,2,1,0:T(8,128)(2,1)S(1)}, bf16[2,4,256,128]{3,2,1,0:T(8,128)(2,1)S(1)}, u32[]{:S(2)}, u32[]{:S(2)}) collective-permute-start(bf16[2,4,256,128]{3,2,1,0:T(8,128)(2,1)S(1)} %maximum_bitcast_fusion.kv_ref), channel_id=1, source_target_pairs={{0,2},{1,3},{2,4},{3,5},{4,6},{5,7},{6,8},{7,9},{8,10},{9,11},{10,... | collective-permute-start | bytes 1572872 | tf_op jit(solution)/shard_map/ppermute | solution.py:143
  27.3 1.3 %collective-permute-start.3 = (bf16[2,4,256,128]{3,2,1,0:T(8,128)(2,1)S(1)}, bf16[2,4,256,128]{3,2,1,0:T(8,128)(2,1)S(1)}, u32[]{:S(2)}, u32[]{:S(2)}) collective-permute-start(bf16[2,4,256,128]{3,2,1,0:T(8,128)(2,1)S(1)} %maximum_bitcast_fusion.kv_ref), channel_id=1, source_target_pairs={{0,225},{2,227},{4,229},{6,231},{8,233},{10,235},{12,237},{14,239}... | collective-permute-start | bytes 1572872 | tf_op jit(solution)/shard_map/ppermute | solution.py:143
  28.6 6.4 %collective-permute-start.4 = (bf16[2,4,256,128]{3,2,1,0:T(8,128)(2,1)S(1)}, bf16[2,4,256,128]{3,2,1,0:T(8,128)(2,1)}, u32[]{:S(2)}, u32[]{:S(2)}) collective-permute-start(bf16[2,4,256,128]{3,2,1,0:T(8,128)(2,1)S(1)} %collective-permute-done.far_ref), channel_id=1, source_target_pairs={{1,0},{3,2},{5,4},{7,6},{9,8},{11,10},{13,12},{15,14},{17,16},{19,... | collective-permute-start | bytes 1572872 | tf_op jit(solution)/shard_map/ppermute | solution.py:143
  35.1 2.0 %collective-permute-done.1.far_ref = bf16[2,4,256,128]{3,2,1,0:T(8,128)(2,1)S(1)} collective-permute-done((bf16[2,4,256,128]{3,2,1,0:T(8,128)(2,1)S(1)}, bf16[2,4,256,128]{3,2,1,0:T(8,128)(2,1)S(1)}, u32[]{:S(2)}, u32[]{:S(2)}) %collective-permute-start.1) | collective-permute-done | bytes 524320 | tf_op jit(solution)/shard_map/ppermute | solution.py:143
  37.1 0.1 broadcast_select_fusion
  37.1 2.5 %collective-permute-start.2 = (bf16[2,4,256,128]{3,2,1,0:T(8,128)(2,1)S(1)}, bf16[2,4,256,128]{3,2,1,0:T(8,128)(2,1)}, u32[]{:S(2)}, u32[]{:S(2)}) collective-permute-start(bf16[2,4,256,128]{3,2,1,0:T(8,128)(2,1)S(1)} %broadcast_select_fusion), channel_id=1, source_target_pairs={{0,1},{1,0},{2,3},{3,2},{4,5},{5,4},{6,7},{7,6},{8,9},{9,8},{10,11... | collective-permute-start | bytes 1572872 | tf_op jit(solution)/shard_map/ppermute | solution.py:143
  39.6 0.8 multiply_bitcast_fusion
  40.4 0.2 copy.15
  40.6 0.9 reshape.18.lse_ref
  41.5 0.2 copy.16
  41.7 0.9 reshape.19.dot_ref
  42.6 0.8 copy-done.5
  43.4 14.6 %partner.1 = (f32[256,32,128]{2,1,0:T(8,128)}, bf16[2,4,256,128]{3,2,1,0:T(8,128)(2,1)}, f32[2,4,256,128]{3,2,1,0:T(8,128)}) custom-call(bf16[256,32,128]{2,1,0:T(8,128)(2,1)} %bitcast.17, bf16[256,32,128]{2,1,0:T(8,128)(2,1)} %bitcast.20, f32[4,1,2048]{2,1,0:T(1,128)} %reshape.18.lse_ref, f32[4,1,2048]{2,1,0:T(1,128)} %reshape.19.dot_ref, ...), custom_call_target="tpu_custom_call" | custom-call | flops 5368709120 | bytes 16777216 | tf_op jit(solution)/shard_map/partner/pallas_call | solution.py:98
  58.0 1.3 %collective-permute-start.7 = (bf16[2,4,256,128]{3,2,1,0:T(8,128)(2,1)}, bf16[2,4,256,128]{3,2,1,0:T(8,128)(2,1)S(1)}, u32[]{:S(2)}, u32[]{:S(2)}) collective-permute-start(bf16[2,4,256,128]{3,2,1,0:T(8,128)(2,1)} %get-tuple-element.18), channel_id=1, source_target_pairs={{0,1},{2,3},{4,5},{6,7},{8,9},{10,11},{12,13},{14,15},{16,17},{18,... | collective-permute-start | bytes 1572872 | tf_op jit(solution)/shard_map/ppermute | solution.py:143
  59.3 15.1 %earlier.1 = (f32[256,32,128]{2,1,0:T(8,128)}, bf16[2,4,256,128]{3,2,1,0:T(8,128)(2,1)}, f32[2,4,256,128]{3,2,1,0:T(8,128)}) custom-call(bf16[256,32,128]{2,1,0:T(8,128)(2,1)} %bitcast.18, bf16[256,32,128]{2,1,0:T(8,128)(2,1)} %bitcast.21, f32[4,1,2048]{2,1,0:T(1,128)} %reshape.18.lse_ref, f32[4,1,2048]{2,1,0:T(1,128)} %reshape.19.dot_ref, ...), custom_call_target="tpu_custom_call" | custom-call | flops 5368709120 | bytes 16777216 | tf_op jit(solution)/shard_map/earlier/pallas_call | solution.py:98
  74.4 1.2 collective-permute-start.5
  75.6 3.0 %collective-permute-start.6 = (bf16[2,4,256,128]{3,2,1,0:T(8,128)(2,1)}, bf16[2,4,256,128]{3,2,1,0:T(8,128)(2,1)S(1)}, u32[]{:S(2)}, u32[]{:S(2)}) collective-permute-start(bf16[2,4,256,128]{3,2,1,0:T(8,128)(2,1)} %get-tuple-element.18), channel_id=1, source_target_pairs={{1,32},{3,34},{5,36},{7,38},{9,40},{11,42},{13,44},{15,46},{17,48}... | collective-permute-start | bytes 1572872 | tf_op jit(solution)/shard_map/ppermute | solution.py:143
  78.6 0.1 add_convert_fusion
  78.8 3.7 %collective-permute-start.8 = (bf16[2,4,256,128]{3,2,1,0:T(8,128)(2,1)S(1)}, bf16[2,4,256,128]{3,2,1,0:T(8,128)(2,1)S(1)}, u32[]{:S(2)}, u32[]{:S(2)}) collective-permute-start(bf16[2,4,256,128]{3,2,1,0:T(8,128)(2,1)S(1)} %add_convert_fusion), channel_id=1, source_target_pairs={{2,32},{3,33},{4,34},{5,35},{6,36},{7,37},{8,38},{9,39},{10,40},{1... | collective-permute-start | bytes 1572872 | tf_op jit(solution)/shard_map/ppermute | solution.py:143
  82.4 1.4 %fusion.6 = bf16[2,4,256,128]{3,2,1,0:T(8,128)(2,1)S(1)} fusion(f32[2,4,256,128]{3,2,1,0:T(8,128)} %get-tuple-element.20, bf16[2,4,256,128]{3,2,1,0:T(8,128)(2,1)S(1)} %collective-permute-done.5, pred[]{:T(512)S(6)} %eq.5), kind=kLoop, calls=%fused_computation.8 | loop fusion | flops 1048576 | bytes 2097153 | tf_op jit(solution)/shard_map/convert_element_type | solution.py:198
  83.8 1.9 %collective-permute-start.9 = (bf16[2,4,256,128]{3,2,1,0:T(8,128)(2,1)S(1)}, bf16[2,4,256,128]{3,2,1,0:T(8,128)(2,1)S(1)}, u32[]{:S(2)}, u32[]{:S(2)}) collective-permute-start(bf16[2,4,256,128]{3,2,1,0:T(8,128)(2,1)S(1)} %fusion.6), channel_id=1, source_target_pairs={{2,0},{3,1},{4,2},{5,3},{6,4},{7,5},{8,6},{9,7},{10,8},{11,9},{12,... | collective-permute-start | bytes 1572872 | tf_op jit(solution)/shard_map/ppermute | solution.py:143
  85.7 10.6 %own.1 = (f32[256,32,128]{2,1,0:T(8,128)}, f32[2,4,256,128]{3,2,1,0:T(8,128)}) custom-call(bf16[256,32,128]{2,1,0:T(8,128)(2,1)} %bitcast.19, bf16[256,32,128]{2,1,0:T(8,128)(2,1)} %bitcast.22, f32[4,1,2048]{2,1,0:T(1,128)} %reshape.18.lse_ref, f32[4,1,2048]{2,1,0:T(1,128)} %reshape.19.dot_ref, bf16[2,4,256,128]{3,2,1,0:T(8,128)(2,1)} %copy-done.1, ...), custom_call_target="tpu_custom_call" | custom-call | flops 2684354560 | bytes 16777216 | tf_op jit(solution)/shard_map/own/pallas_call | solution.py:121
  96.3 13.3 %collective-permute-done.8 = bf16[2,4,256,128]{3,2,1,0:T(8,128)(2,1)S(1)} collective-permute-done((bf16[2,4,256,128]{3,2,1,0:T(8,128)(2,1)S(1)}, bf16[2,4,256,128]{3,2,1,0:T(8,128)(2,1)S(1)}, u32[]{:S(2)}, u32[]{:S(2)}) %collective-permute-start.8) | collective-permute-done | bytes 524320 | tf_op jit(solution)/shard_map/ppermute | solution.py:143
  109.7 6.2 %collective-permute-done.9 = bf16[2,4,256,128]{3,2,1,0:T(8,128)(2,1)S(1)} collective-permute-done((bf16[2,4,256,128]{3,2,1,0:T(8,128)(2,1)S(1)}, bf16[2,4,256,128]{3,2,1,0:T(8,128)(2,1)S(1)}, u32[]{:S(2)}, u32[]{:S(2)}) %collective-permute-start.9) | collective-permute-done | bytes 524320 | tf_op jit(solution)/shard_map/ppermute | solution.py:143
  115.9 1.5 %fusion.4 = f32[2,256,4,128]{3,1,2,0:T(8,128)S(1)} fusion(f32[2,4,256,128]{3,2,1,0:T(8,128)} %get-tuple-element.16, bf16[2,4,256,128]{3,2,1,0:T(8,128)(2,1)S(1)} %collective-permute-done.5, bf16[2,4,256,128]{3,2,1,0:T(8,128)(2,1)S(1)} %collective-permute-done.9, bf16[2,4,256,128]{3,2,1,0:T(8,128)(2,1)S(1)} %collective-permute-done.8, ...), kind=kLoop, calls=%fused_computation.6 | loop fusion | flops 2359296 | bytes 4194305 | tf_op jit(solution)/shard_map/transpose | solution.py:203
  117.4 0.1 fusion.7
  117.5 1.1 copy.26
  118.6 1.1 copy.25
  (18 shorter events, 0.1 us)
Async XLA Ops:
  0.6 40.9 %copy-start.3 = (f32[1,32,256]{2,1,0:T(8,128)S(1)}, f32[1,32,256]{2,1,0:T(8,128)}, u32[]{:S(2)}) copy-start(f32[1,32,256]{2,1,0:T(8,128)} %param.11) | copy-start | bytes 98308
  2.7 55.3 %copy-start.1 = (bf16[2,4,256,128]{3,2,1,0:T(8,128)(2,1)}, bf16[2,4,256,128]{3,2,1,0:T(8,128)(2,1)S(1)}, u32[]{:S(2)}) copy-start(bf16[2,4,256,128]{3,2,1,0:T(8,128)(2,1)S(1)} %maximum_bitcast_fusion.kv_ref) | copy-start | bytes 1572868
  2.7 17.2 %collective-permute-start = (bf16[2,4,256,128]{3,2,1,0:T(8,128)(2,1)S(1)}, bf16[2,4,256,128]{3,2,1,0:T(8,128)(2,1)S(1)}, u32[]{:S(2)}, u32[]{:S(2)}) collective-permute-start(bf16[2,4,256,128]{3,2,1,0:T(8,128)(2,1)S(1)} %maximum_bitcast_fusion.kv_ref), channel_id=1, source_target_pairs={{0,226},{1,227},{2,228},{3,229},{4,230},{5,231},{6,232},{7,233},{8... | collective-permute-start | bytes 1572872 | tf_op jit(solution)/shard_map/ppermute | solution.py:143
  19.9 22.7 %copy-start.4 = (bf16[2,4,256,128]{3,2,1,0:T(8,128)(2,1)}, bf16[2,4,256,128]{3,2,1,0:T(8,128)(2,1)S(1)}, u32[]{:S(2)}) copy-start(bf16[2,4,256,128]{3,2,1,0:T(8,128)(2,1)S(1)} %collective-permute-done.far_ref) | copy-start | bytes 1572868
  19.9 17.2 %collective-permute-start.1 = (bf16[2,4,256,128]{3,2,1,0:T(8,128)(2,1)S(1)}, bf16[2,4,256,128]{3,2,1,0:T(8,128)(2,1)S(1)}, u32[]{:S(2)}, u32[]{:S(2)}) collective-permute-start(bf16[2,4,256,128]{3,2,1,0:T(8,128)(2,1)S(1)} %maximum_bitcast_fusion.kv_ref), channel_id=1, source_target_pairs={{0,2},{1,3},{2,4},{3,5},{4,6},{5,7},{6,8},{7,9},{8,10},{9,11},{10,... | collective-permute-start | bytes 1572872 | tf_op jit(solution)/shard_map/ppermute | solution.py:143
  27.3 15.2 %collective-permute-start.3 = (bf16[2,4,256,128]{3,2,1,0:T(8,128)(2,1)S(1)}, bf16[2,4,256,128]{3,2,1,0:T(8,128)(2,1)S(1)}, u32[]{:S(2)}, u32[]{:S(2)}) collective-permute-start(bf16[2,4,256,128]{3,2,1,0:T(8,128)(2,1)S(1)} %maximum_bitcast_fusion.kv_ref), channel_id=1, source_target_pairs={{0,225},{2,227},{4,229},{6,231},{8,233},{10,235},{12,237},{14,239}... | collective-permute-start | bytes 1572872 | tf_op jit(solution)/shard_map/ppermute | solution.py:143
  28.6 13.9 %collective-permute-start.4 = (bf16[2,4,256,128]{3,2,1,0:T(8,128)(2,1)S(1)}, bf16[2,4,256,128]{3,2,1,0:T(8,128)(2,1)}, u32[]{:S(2)}, u32[]{:S(2)}) collective-permute-start(bf16[2,4,256,128]{3,2,1,0:T(8,128)(2,1)S(1)} %collective-permute-done.far_ref), channel_id=1, source_target_pairs={{1,0},{3,2},{5,4},{7,6},{9,8},{11,10},{13,12},{15,14},{17,16},{19,... | collective-permute-start | bytes 1572872 | tf_op jit(solution)/shard_map/ppermute | solution.py:143
  37.1 20.9 %copy-start.2 = (bf16[2,4,256,128]{3,2,1,0:T(8,128)(2,1)}, bf16[2,4,256,128]{3,2,1,0:T(8,128)(2,1)S(1)}, u32[]{:S(2)}) copy-start(bf16[2,4,256,128]{3,2,1,0:T(8,128)(2,1)S(1)} %collective-permute-done.1.far_ref) | copy-start | bytes 1572868
  37.1 22.2 %collective-permute-start.2 = (bf16[2,4,256,128]{3,2,1,0:T(8,128)(2,1)S(1)}, bf16[2,4,256,128]{3,2,1,0:T(8,128)(2,1)}, u32[]{:S(2)}, u32[]{:S(2)}) collective-permute-start(bf16[2,4,256,128]{3,2,1,0:T(8,128)(2,1)S(1)} %broadcast_select_fusion), channel_id=1, source_target_pairs={{0,1},{1,0},{2,3},{3,2},{4,5},{5,4},{6,7},{7,6},{8,9},{9,8},{10,11... | collective-permute-start | bytes 1572872 | tf_op jit(solution)/shard_map/ppermute | solution.py:143
  42.6 0.8 copy-start.5
  58.0 20.6 %collective-permute-start.7 = (bf16[2,4,256,128]{3,2,1,0:T(8,128)(2,1)}, bf16[2,4,256,128]{3,2,1,0:T(8,128)(2,1)S(1)}, u32[]{:S(2)}, u32[]{:S(2)}) collective-permute-start(bf16[2,4,256,128]{3,2,1,0:T(8,128)(2,1)} %get-tuple-element.18), channel_id=1, source_target_pairs={{0,1},{2,3},{4,5},{6,7},{8,9},{10,11},{12,13},{14,15},{16,17},{18,... | collective-permute-start | bytes 1572872 | tf_op jit(solution)/shard_map/ppermute | solution.py:143
  59.3 19.3 %copy-start = (f32[2,4,256,128]{3,2,1,0:T(8,128)S(1)}, f32[2,4,256,128]{3,2,1,0:T(8,128)}, u32[]{:S(2)}) copy-start(f32[2,4,256,128]{3,2,1,0:T(8,128)} %get-tuple-element.19) | copy-start | bytes 3145732
  74.4 8.0 %collective-permute-start.5 = (bf16[2,4,256,128]{3,2,1,0:T(8,128)(2,1)}, bf16[2,4,256,128]{3,2,1,0:T(8,128)(2,1)S(1)}, u32[]{:S(2)}, u32[]{:S(2)}) collective-permute-start(bf16[2,4,256,128]{3,2,1,0:T(8,128)(2,1)} %get-tuple-element.17), channel_id=1, source_target_pairs={{0,1},{1,0},{2,3},{3,2},{4,5},{5,4},{6,7},{7,6},{8,9},{9,8},{10,11... | collective-permute-start | bytes 1572872 | tf_op jit(solution)/shard_map/ppermute | solution.py:143
  75.6 20.8 %collective-permute-start.6 = (bf16[2,4,256,128]{3,2,1,0:T(8,128)(2,1)}, bf16[2,4,256,128]{3,2,1,0:T(8,128)(2,1)S(1)}, u32[]{:S(2)}, u32[]{:S(2)}) collective-permute-start(bf16[2,4,256,128]{3,2,1,0:T(8,128)(2,1)} %get-tuple-element.18), channel_id=1, source_target_pairs={{1,32},{3,34},{5,36},{7,38},{9,40},{11,42},{13,44},{15,46},{17,48}... | collective-permute-start | bytes 1572872 | tf_op jit(solution)/shard_map/ppermute | solution.py:143
  78.8 30.9 %collective-permute-start.8 = (bf16[2,4,256,128]{3,2,1,0:T(8,128)(2,1)S(1)}, bf16[2,4,256,128]{3,2,1,0:T(8,128)(2,1)S(1)}, u32[]{:S(2)}, u32[]{:S(2)}) collective-permute-start(bf16[2,4,256,128]{3,2,1,0:T(8,128)(2,1)S(1)} %add_convert_fusion), channel_id=1, source_target_pairs={{2,32},{3,33},{4,34},{5,35},{6,36},{7,37},{8,38},{9,39},{10,40},{1... | collective-permute-start | bytes 1572872 | tf_op jit(solution)/shard_map/ppermute | solution.py:143
  83.8 32.1 %collective-permute-start.9 = (bf16[2,4,256,128]{3,2,1,0:T(8,128)(2,1)S(1)}, bf16[2,4,256,128]{3,2,1,0:T(8,128)(2,1)S(1)}, u32[]{:S(2)}, u32[]{:S(2)}) collective-permute-start(bf16[2,4,256,128]{3,2,1,0:T(8,128)(2,1)S(1)} %fusion.6), channel_id=1, source_target_pairs={{2,0},{3,1},{4,2},{5,3},{6,4},{7,5},{8,6},{9,7},{10,8},{11,9},{12,... | collective-permute-start | bytes 1572872 | tf_op jit(solution)/shard_map/ppermute | solution.py:143

commit v2 on v1

v2 whole, which is shorter than its diff:
```python
import functools
import math

import jax
import jax.numpy as jnp
from jax import lax
from jax.experimental import pallas as pl
from jax.experimental.pallas import tpu as pltpu
from jax.sharding import PartitionSpec as P


LOG2E = math.log2(math.e)
F32, BF16 = jnp.float32, jnp.bfloat16
NT = (((1,), (1,)), ((), ()))
NN = (((1,), (0,)), ((), ()))
TN = (((0,), (0,)), ((), ()))


def mm(a, b, dims):
    return lax.dot_general(a, b, dims, preferred_element_type=F32)


def columns(width, q, g, lse_ref, dot_ref, sl, k, v, mask):
    qc, gc = q[sl, :], g[sl, :]
    s = mm(k, qc, NT)
    p = jnp.exp2(s * (LOG2E * width**-0.5) - lse_ref[0, :, sl])
    if mask is not None:
        p = jnp.where(mask, p, 0.0)
    dv = mm(p.astype(BF16), gc, NN)
    dp = mm(v, gc, NT)
    ds = (p * (dp - dot_ref[0, :, sl])).astype(BF16)
    dk = mm(ds, qc, NN)
    dq = mm(ds, k, TN)
    return dq, dk, dv


def earlier_kernel(cw, merge, last, q_ref, g_ref, lse_ref, dot_ref, prev_ref, *rest):
    n_in = sum(merge)
    in_refs, dq_ref, outs = rest[:n_in], rest[n_in], rest[n_in + 1 :]
    tokens, heads, width = q_ref.shape
    n = tokens * heads
    q, g = q_ref.reshape(n, width), g_ref.reshape(n, width)
    blocks = []
    for count in merge:
        k, v = in_refs[0][0, 0], in_refs[0][1, 0]
        for other in in_refs[1:count]:
            k, v = k + other[0, 0], v + other[1, 0]
        blocks.append((k, v))
        in_refs = in_refs[count:]
    k = jnp.concatenate([k for k, _ in blocks], axis=0)
    v = jnp.concatenate([v for _, v in blocks], axis=0)
    dk = dv = None
    for c in range(n // cw):
        sl = pl.ds(c * cw, cw)
        dqc, dkc, dvc = columns(width, q, g, lse_ref, dot_ref, sl, k, v, None)
        dqc = dqc + prev_ref.reshape(n, width)[sl, :]
        dq_ref.reshape(n, width)[sl, :] = dqc * width**-0.5 if last else dqc
        dk = dkc if dk is None else dk + dkc
        dv = dvc if dv is None else dv + dvc
    dk = dk * width**-0.5
    for i, out in enumerate(outs):
        out[0, 0] = dk[i * tokens : (i + 1) * tokens].astype(BF16)
        out[1, 0] = dv[i * tokens : (i + 1) * tokens].astype(BF16)


def own_kernel(cw, step, q_ref, g_ref, lse_ref, dot_ref, kv_ref, dq_ref, own_out):
    tokens, heads, width = q_ref.shape
    n = tokens * heads
    q, g = q_ref.reshape(n, width), g_ref.reshape(n, width)
    parts = []
    for c in range(n // cw):
        sl = pl.ds(c * cw, cw)
        seen = pl.cdiv((c + 1) * cw // heads, step) * step
        k, v = kv_ref[0, 0, :seen, :], kv_ref[1, 0, :seen, :]
        key = lax.broadcasted_iota(jnp.int32, (seen, cw), 0)
        column = lax.broadcasted_iota(jnp.int32, (seen, cw), 1) + c * cw
        dqc, dkc, dvc = columns(width, q, g, lse_ref, dot_ref, sl, k, v, key * heads <= column)
        dq_ref.reshape(n, width)[sl, :] = dqc
        parts.append((dkc * width**-0.5, dvc))
    done = 0
    for seen in sorted({dk.shape[0] for dk, _ in parts}):
        rows = [(dk[done:seen], dv[done:seen]) for dk, dv in parts if dk.shape[0] >= seen]
        own_out[0, 0, done:seen, :] = sum(dk for dk, _ in rows)
        own_out[1, 0, done:seen, :] = sum(dv for _, dv in rows)
        done = seen


def specs(tokens, heads, groups, width):
    per = heads // groups
    row = pl.BlockSpec((tokens, per, width), lambda j: (0, j, 0))
    vec = pl.BlockSpec((1, 1, tokens * per), lambda j: (j, 0, 0))
    blk = pl.BlockSpec((2, 1, tokens, width), lambda j: (0, j, 0, 0))
    return row, vec, blk


def earlier_call(q, g, lse, dots, prev, blocks, last):
    tokens, heads, width = q.shape
    groups = blocks[0][0].shape[1]
    row, vec, blk = specs(tokens, heads, groups, width)
    pairs = len(blocks) * tokens * heads * tokens
    parts = [part for block in blocks for part in block]
    merge = tuple(len(block) for block in blocks)
    return pl.pallas_call(
        functools.partial(earlier_kernel, 512 if len(blocks) > 1 else 1024, merge, last),
        grid=(groups,),
        in_specs=[row, row, vec, vec, row] + [blk] * len(parts),
        out_specs=[row] + [blk] * len(blocks),
        out_shape=[jax.ShapeDtypeStruct(q.shape, F32)]
        + [jax.ShapeDtypeStruct(parts[0].shape, BF16)] * len(blocks),
        compiler_params=pltpu.CompilerParams(dimension_semantics=("arbitrary",)),
        cost_estimate=pl.CostEstimate(
            flops=10 * pairs * width, transcendentals=pairs, bytes_accessed=16 << 20
        ),
    )(q, g, lse, dots, prev, *parts)


def own_call(q, g, lse, dots, kv):
    tokens, heads, width = q.shape
    groups = kv.shape[1]
    row, vec, blk = specs(tokens, heads, groups, width)
    pairs = tokens * heads * tokens
    return pl.pallas_call(
        functools.partial(own_kernel, 1024, 128),
        grid=(groups,),
        in_specs=[row, row, vec, vec, blk],
        out_specs=[row, blk],
        out_shape=[jax.ShapeDtypeStruct(q.shape, F32), jax.ShapeDtypeStruct(kv.shape, F32)],
        compiler_params=pltpu.CompilerParams(dimension_semantics=("arbitrary",)),
        cost_estimate=pl.CostEstimate(
            flops=10 * pairs * width, transcendentals=pairs, bytes_accessed=16 << 20
        ),
        name="own",
    )(q, g, lse, dots, kv)


def send(x, by_doc, to):
    docs, ctxs = lax.axis_size("doc"), lax.axis_size("ctx")
    pairs = []
    for d in range(docs):
        for c in range(ctxs):
            t = to(c)
            if t is not None and 0 <= t < ctxs:
                pairs.append((d * ctxs + c, (d + by_doc) % docs * ctxs + t))
    return lax.ppermute(x, ("doc", "ctx"), pairs)


def ahead(c):
    return c + 2


def back_one(c):
    return c - 1


def back_two(c):
    return c - 2


def swap(c):
    return c ^ 1


def even_to_odd(c):
    return c + 1 if c % 2 == 0 else None


def odd_to_even(c):
    return c - 1 if c % 2 == 1 else None


def by_group(x, groups):
    heads, tokens = x.shape
    return x.reshape(groups, heads // groups, tokens).transpose(0, 2, 1).reshape(groups, 1, -1)


def step(queries, stored_key_state, stored_value_state, out_grad, logsumexp, row_dots):
    groups = stored_key_state.shape[2]
    q, g = queries[0], out_grad[0]
    odd = lax.axis_index("ctx") % 2 == 1
    kv = jnp.stack([stored_key_state[0], stored_value_state[0]]).transpose(0, 2, 1, 3)

    part_far = send(kv, -1, ahead)
    part_near_odd = send(kv, -1, even_to_odd)
    own_far = send(kv, 0, ahead)
    part_near_even = send(part_far, 0, odd_to_even)

    lse = by_group(logsumexp[0] * LOG2E, groups)
    dots = by_group(row_dots[0], groups)
    dq, own_grad = own_call(q, g, lse, dots, kv)
    dq, far_grad, near_grad = earlier_call(
        q, g, lse, dots, dq, [[part_far], [part_near_odd, part_near_even]], False
    )
    own_far, dq = lax.optimization_barrier((own_far, dq))
    part_far_home = send(far_grad, 1, back_two)
    part_near_home = send(near_grad, 1, back_one)
    own_near = send(jnp.where(odd, own_far, kv), 0, swap)
    dq, far_grad = earlier_call(q, g, lse, dots, dq, [[own_far]], False)
    own_far_home = send(far_grad, 0, back_two)
    dq, near_grad = earlier_call(q, g, lse, dots, dq, [[own_near]], True)
    own_near_home = send(near_grad, 0, back_one)

    total = own_grad + part_far_home.astype(F32) + part_near_home.astype(F32)
    total = total + own_far_home.astype(F32) + own_near_home.astype(F32)
    total = total.transpose(0, 2, 1, 3)
    return dq[None], total[0][None], total[1][None]


def solution(mesh):
    rows, vecs = P("doc", "ctx", None, None), P("doc", None, "ctx")
    return jax.shard_map(
        step,
        mesh=mesh,
        in_specs=(rows, rows, rows, rows, vecs, vecs),
        out_specs=(rows, rows, rows),
        check_vma=False,
    )
```

time: 120 us -> 123 us (1.025)
  waiting for transfers between devices: 32.1 us -> 38.8 us
  starting transfers between devices: 35.3 us -> 29.9 us
  other arithmetic: 3.9 us -> 1.18 us
  Pallas kernels: 40.3 us -> 42.5 us
  local copies, waits for them, and re-layouts: 7.3 us -> 9.45 us
    ppermute x10 -> x9, waiting for transfers between devices: 32.1 us -> 38.8 us  [send(): return lax.ppermute(x, ('doc', 'ctx'), pairs)]
    ppermute x10 -> x9, starting transfers between devices: 35.3 us -> 29.9 us  [send(): return lax.ppermute(x, ('doc', 'ctx'), pairs)]
    pallas_call x3 -> x4, Pallas kernels: 40.3 us -> 42.5 us  [the longest x3 34 us: earlier_call(): pl.pallas_call(functools.partial(earlier_kernel, 512 if len(blocks) > 1 e...]
    convert_element_type x2 -> x0, other arithmetic: 1.48 us -> none  [the longest x1 1.37 us: per_device(): (own_far_grad + jnp.where(odd, swapped, 0.0)).astype(BF16)]
    unnamed x16 -> x18, local copies, waits for them, and re-layouts: 5.05 us -> 6.42 us
    transpose x2, other arithmetic: 1.59 us -> 0.35 us  [the longest x1 0.29 us: step(): total = total.transpose(0, 2, 1, 3)]
  transfers between devices with their start and end apart: 10 -> 9, of which waited for: 4 -> 5; matrix products, arithmetic and copies ran while one was open for 4% -> 3% of each run, Pallas kernels for 34% -> 35%
where the time goes in v2:
time: 123 us
  Pallas kernels  42.5 us (35%)
  waiting for transfers between devices  38.8 us (32%)
  starting transfers between devices  29.9 us (24%)
  local copies, waits for them, and re-layouts  9.45 us (8%)
    ppermute x9, waiting for transfers between devices, send(): return lax.ppermute(x, ('doc', 'ctx'), pairs)  38.8 us
    pallas_call x3, Pallas kernels, earlier_call(): pl.pallas_call(functools.partial(earlier_kernel, 512 if len(blocks) > 1 e...  34 us
    ppermute x9, starting transfers between devices, send(): return lax.ppermute(x, ('doc', 'ctx'), pairs)  29.9 us
    pallas_call x1, Pallas kernels, own_call(): pl.pallas_call(functools.partial(own_kernel, 1024, 128), grid=(groups,),...  8.5 us
    unnamed x18, local copies, waits for them, and re-layouts  6.42 us
  transfers between devices with their start and end apart: 9, of which 5 were waited for; matrix products, arithmetic and copies ran while one was open for 3% of the time, Pallas kernels for 35%

profile of v2, /device:TPU:121, one launch (start us, length us, event | category | flops | bytes accessed | tf_op | source)
XLA Modules:
  0.0 122.6 jit_solution(15928433843166259790)
XLA Ops:
  0.6 1.0 copy.17
  1.6 1.0 copy.18
  2.7 6.6 %collective-permute-start.1 = (bf16[2,4,256,128]{3,2,1,0:T(8,128)(2,1)S(1)}, bf16[2,4,256,128]{3,2,1,0:T(8,128)(2,1)S(1)}, u32[]{:S(2)}, u32[]{:S(2)}) collective-permute-start(bf16[2,4,256,128]{3,2,1,0:T(8,128)(2,1)S(1)} %maximum_bitcast_fusion.kv_ref), channel_id=1, source_target_pairs={{0,226},{1,227},{2,228},{3,229},{4,230},{5,231},{6,232},{7,233},{8... | collective-permute-start | bytes 1572872 | tf_op jit(solution)/shard_map/ppermute | solution.py:144
  9.3 1.3 %collective-permute-start.2 = (bf16[2,4,256,128]{3,2,1,0:T(8,128)(2,1)S(1)}, bf16[2,4,256,128]{3,2,1,0:T(8,128)(2,1)S(1)}, u32[]{:S(2)}, u32[]{:S(2)}) collective-permute-start(bf16[2,4,256,128]{3,2,1,0:T(8,128)(2,1)S(1)} %maximum_bitcast_fusion.kv_ref), channel_id=1, source_target_pairs={{0,225},{2,227},{4,229},{6,231},{8,233},{10,235},{12,237},{14,239}... | collective-permute-start | bytes 1572872 | tf_op jit(solution)/shard_map/ppermute | solution.py:144
  10.6 9.3 %collective-permute-done.1.rest_0_ = bf16[2,4,256,128]{3,2,1,0:T(8,128)(2,1)S(1)} collective-permute-done((bf16[2,4,256,128]{3,2,1,0:T(8,128)(2,1)S(1)}, bf16[2,4,256,128]{3,2,1,0:T(8,128)(2,1)S(1)}, u32[]{:S(2)}, u32[]{:S(2)}) %collective-permute-start.1) | collective-permute-done | bytes 524320 | tf_op jit(solution)/shard_map/ppermute | solution.py:144
  19.9 4.2 %collective-permute-start.3 = (bf16[2,4,256,128]{3,2,1,0:T(8,128)(2,1)S(1)}, bf16[2,4,256,128]{3,2,1,0:T(8,128)(2,1)}, u32[]{:S(2)}, u32[]{:S(2)}) collective-permute-start(bf16[2,4,256,128]{3,2,1,0:T(8,128)(2,1)S(1)} %collective-permute-done.1.rest_0_), channel_id=1, source_target_pairs={{1,0},{3,2},{5,4},{7,6},{9,8},{11,10},{13,12},{15,14},{17,16},{19,... | collective-permute-start | bytes 1572872 | tf_op jit(solution)/shard_map/ppermute | solution.py:144
  24.2 7.5 %collective-permute-start = (bf16[2,4,256,128]{3,2,1,0:T(8,128)(2,1)S(1)}, bf16[2,4,256,128]{3,2,1,0:T(8,128)(2,1)S(1)}, u32[]{:S(2)}, u32[]{:S(2)}) collective-permute-start(bf16[2,4,256,128]{3,2,1,0:T(8,128)(2,1)S(1)} %maximum_bitcast_fusion.kv_ref), channel_id=1, source_target_pairs={{0,2},{1,3},{2,4},{3,5},{4,6},{5,7},{6,8},{7,9},{8,10},{9,11},{10,... | collective-permute-start | bytes 1572872 | tf_op jit(solution)/shard_map/ppermute | solution.py:144
  31.6 0.8 multiply_bitcast_fusion
  32.4 0.2 copy.15
  32.6 0.9 reshape.18.lse_ref
  33.5 0.9 copy.16
  34.5 0.9 reshape.19.dot_ref
  35.4 8.5 %own.1 = (f32[256,32,128]{2,1,0:T(8,128)}, f32[2,4,256,128]{3,2,1,0:T(8,128)}) custom-call(bf16[256,32,128]{2,1,0:T(8,128)(2,1)} %bitcast.17, bf16[256,32,128]{2,1,0:T(8,128)(2,1)} %bitcast.21, f32[4,1,2048]{2,1,0:T(1,128)} %reshape.18.lse_ref, f32[4,1,2048]{2,1,0:T(1,128)} %reshape.19.dot_ref, bf16[2,4,256,128]{3,2,1,0:T(8,128)(2,1)} %copy-done.1), custom_call_target="tpu_custom_call" | custom-call | flops 2684354560 | bytes 16777216 | tf_op jit(solution)/shard_map/own/pallas_call | solution.py:122
  43.9 0.8 copy-done.4
  44.7 15.1 %shard_map.85 = (f32[256,32,128]{2,1,0:T(8,128)}, bf16[2,4,256,128]{3,2,1,0:T(8,128)(2,1)}, bf16[2,4,256,128]{3,2,1,0:T(8,128)(2,1)}) custom-call(bf16[256,32,128]{2,1,0:T(8,128)(2,1)} %bitcast.18, bf16[256,32,128]{2,1,0:T(8,128)(2,1)} %bitcast.22, f32[4,1,2048]{2,1,0:T(1,128)} %reshape.18.lse_ref, f32[4,1,2048]{2,1,0:T(1,128)} %reshape.19.dot_ref, ...), custom_call_target="tpu_custom_call" | custom-call | flops 5368709120 | bytes 16777216 | tf_op jit(solution)/shard_map/pallas_call | solution.py:103
  59.8 0.1 broadcast_select_fusion
  59.9 0.1 collective-permute-start.4
  60.0 0.6 copy-done.2
  60.5 9.4 %shard_map.86 = (f32[256,32,128]{2,1,0:T(8,128)}, bf16[2,4,256,128]{3,2,1,0:T(8,128)(2,1)}) custom-call(bf16[256,32,128]{2,1,0:T(8,128)(2,1)} %bitcast.19, bf16[256,32,128]{2,1,0:T(8,128)(2,1)} %bitcast.23, f32[4,1,2048]{2,1,0:T(1,128)} %reshape.18.lse_ref, f32[4,1,2048]{2,1,0:T(1,128)} %reshape.19.dot_ref, f32[256,32,128]{2,1,0:T(8,128)} %get-tuple-element.16.prev_ref, ...), custom_call_target="tpu_custom_call" | custom-call | flops 2684354560 | bytes 16777216 | tf_op jit(solution)/shard_map/pallas_call | solution.py:103
  70.0 1.9 %collective-permute-start.7 = (bf16[2,4,256,128]{3,2,1,0:T(8,128)(2,1)}, bf16[2,4,256,128]{3,2,1,0:T(8,128)(2,1)S(1)}, u32[]{:S(2)}, u32[]{:S(2)}) collective-permute-start(bf16[2,4,256,128]{3,2,1,0:T(8,128)(2,1)} %get-tuple-element.23), channel_id=1, source_target_pairs={{2,0},{3,1},{4,2},{5,3},{6,4},{7,5},{8,6},{9,7},{10,8},{11,9},{12,... | collective-permute-start | bytes 1572872 | tf_op jit(solution)/shard_map/ppermute | solution.py:144
  71.9 2.9 %collective-permute-start.5 = (bf16[2,4,256,128]{3,2,1,0:T(8,128)(2,1)}, bf16[2,4,256,128]{3,2,1,0:T(8,128)(2,1)S(1)}, u32[]{:S(2)}, u32[]{:S(2)}) collective-permute-start(bf16[2,4,256,128]{3,2,1,0:T(8,128)(2,1)} %get-tuple-element.21), channel_id=1, source_target_pairs={{2,32},{3,33},{4,34},{5,35},{6,36},{7,37},{8,38},{9,39},{10,40},{1... | collective-permute-start | bytes 1572872 | tf_op jit(solution)/shard_map/ppermute | solution.py:144
  74.8 3.5 %collective-permute-start.6 = (bf16[2,4,256,128]{3,2,1,0:T(8,128)(2,1)S(1)}, bf16[2,4,256,128]{3,2,1,0:T(8,128)(2,1)S(1)}, u32[]{:S(2)}, u32[]{:S(2)}) collective-permute-start(bf16[2,4,256,128]{3,2,1,0:T(8,128)(2,1)S(1)} %copy-done.5), channel_id=1, source_target_pairs={{1,32},{2,33},{3,34},{4,35},{5,36},{6,37},{7,38},{8,39},{9,40},{10... | collective-permute-start | bytes 1572872 | tf_op jit(solution)/shard_map/ppermute | solution.py:144
  78.3 0.8 copy-done.6
  79.1 9.5 %shard_map.87 = (f32[256,32,128]{2,1,0:T(8,128)}, bf16[2,4,256,128]{3,2,1,0:T(8,128)(2,1)}) custom-call(bf16[256,32,128]{2,1,0:T(8,128)(2,1)} %bitcast.20, bf16[256,32,128]{2,1,0:T(8,128)(2,1)} %bitcast.24, f32[4,1,2048]{2,1,0:T(1,128)} %reshape.18.lse_ref, f32[4,1,2048]{2,1,0:T(1,128)} %reshape.19.dot_ref, f32[256,32,128]{2,1,0:T(8,128)} %get-tuple-element.18.prev_ref, ...), custom_call_target="tpu_custom_call" | custom-call | flops 2684354560 | bytes 16777216 | tf_op jit(solution)/shard_map/pallas_call | solution.py:103
  88.6 1.9 %collective-permute-start.8 = (bf16[2,4,256,128]{3,2,1,0:T(8,128)(2,1)}, bf16[2,4,256,128]{3,2,1,0:T(8,128)(2,1)S(1)}, u32[]{:S(2)}, u32[]{:S(2)}) collective-permute-start(bf16[2,4,256,128]{3,2,1,0:T(8,128)(2,1)} %get-tuple-element.24), channel_id=1, source_target_pairs={{1,0},{2,1},{3,2},{4,3},{5,4},{6,5},{7,6},{8,7},{9,8},{10,9},{11,1... | collective-permute-start | bytes 1572872 | tf_op jit(solution)/shard_map/ppermute | solution.py:144
  90.5 6.7 %collective-permute-done.7 = bf16[2,4,256,128]{3,2,1,0:T(8,128)(2,1)S(1)} collective-permute-done((bf16[2,4,256,128]{3,2,1,0:T(8,128)(2,1)}, bf16[2,4,256,128]{3,2,1,0:T(8,128)(2,1)S(1)}, u32[]{:S(2)}, u32[]{:S(2)}) %collective-permute-start.7) | collective-permute-done | bytes 524320 | tf_op jit(solution)/shard_map/ppermute | solution.py:144
  97.3 8.2 %collective-permute-done.5 = bf16[2,4,256,128]{3,2,1,0:T(8,128)(2,1)S(1)} collective-permute-done((bf16[2,4,256,128]{3,2,1,0:T(8,128)(2,1)}, bf16[2,4,256,128]{3,2,1,0:T(8,128)(2,1)S(1)}, u32[]{:S(2)}, u32[]{:S(2)}) %collective-permute-start.5) | collective-permute-done | bytes 524320 | tf_op jit(solution)/shard_map/ppermute | solution.py:144
  105.5 5.8 %collective-permute-done.6 = bf16[2,4,256,128]{3,2,1,0:T(8,128)(2,1)S(1)} collective-permute-done((bf16[2,4,256,128]{3,2,1,0:T(8,128)(2,1)S(1)}, bf16[2,4,256,128]{3,2,1,0:T(8,128)(2,1)S(1)}, u32[]{:S(2)}, u32[]{:S(2)}) %collective-permute-start.6) | collective-permute-done | bytes 524320 | tf_op jit(solution)/shard_map/ppermute | solution.py:144
  111.3 8.7 %collective-permute-done.8 = bf16[2,4,256,128]{3,2,1,0:T(8,128)(2,1)S(1)} collective-permute-done((bf16[2,4,256,128]{3,2,1,0:T(8,128)(2,1)}, bf16[2,4,256,128]{3,2,1,0:T(8,128)(2,1)S(1)}, u32[]{:S(2)}, u32[]{:S(2)}) %collective-permute-start.8) | collective-permute-done | bytes 524320 | tf_op jit(solution)/shard_map/ppermute | solution.py:144
  120.0 0.3 add_bitcast_fusion
  120.3 1.1 copy.27
  121.5 1.1 copy.28
  (17 shorter events, 0.2 us)
Async XLA Ops:
  2.7 32.7 %copy-start.1 = (bf16[2,4,256,128]{3,2,1,0:T(8,128)(2,1)}, bf16[2,4,256,128]{3,2,1,0:T(8,128)(2,1)S(1)}, u32[]{:S(2)}) copy-start(bf16[2,4,256,128]{3,2,1,0:T(8,128)(2,1)S(1)} %maximum_bitcast_fusion.kv_ref) | copy-start | bytes 1572868
  2.7 17.2 %collective-permute-start.1 = (bf16[2,4,256,128]{3,2,1,0:T(8,128)(2,1)S(1)}, bf16[2,4,256,128]{3,2,1,0:T(8,128)(2,1)S(1)}, u32[]{:S(2)}, u32[]{:S(2)}) collective-permute-start(bf16[2,4,256,128]{3,2,1,0:T(8,128)(2,1)S(1)} %maximum_bitcast_fusion.kv_ref), channel_id=1, source_target_pairs={{0,226},{1,227},{2,228},{3,229},{4,230},{5,231},{6,232},{7,233},{8... | collective-permute-start | bytes 1572872 | tf_op jit(solution)/shard_map/ppermute | solution.py:144
  9.3 34.6 %collective-permute-start.2 = (bf16[2,4,256,128]{3,2,1,0:T(8,128)(2,1)S(1)}, bf16[2,4,256,128]{3,2,1,0:T(8,128)(2,1)S(1)}, u32[]{:S(2)}, u32[]{:S(2)}) collective-permute-start(bf16[2,4,256,128]{3,2,1,0:T(8,128)(2,1)S(1)} %maximum_bitcast_fusion.kv_ref), channel_id=1, source_target_pairs={{0,225},{2,227},{4,229},{6,231},{8,233},{10,235},{12,237},{14,239}... | collective-permute-start | bytes 1572872 | tf_op jit(solution)/shard_map/ppermute | solution.py:144
  19.9 24.0 %copy-start.3 = (bf16[2,4,256,128]{3,2,1,0:T(8,128)(2,1)}, bf16[2,4,256,128]{3,2,1,0:T(8,128)(2,1)S(1)}, u32[]{:S(2)}) copy-start(bf16[2,4,256,128]{3,2,1,0:T(8,128)(2,1)S(1)} %collective-permute-done.1.rest_0_) | copy-start | bytes 1572868
  19.9 24.0 %collective-permute-start.3 = (bf16[2,4,256,128]{3,2,1,0:T(8,128)(2,1)S(1)}, bf16[2,4,256,128]{3,2,1,0:T(8,128)(2,1)}, u32[]{:S(2)}, u32[]{:S(2)}) collective-permute-start(bf16[2,4,256,128]{3,2,1,0:T(8,128)(2,1)S(1)} %collective-permute-done.1.rest_0_), channel_id=1, source_target_pairs={{1,0},{3,2},{5,4},{7,6},{9,8},{11,10},{13,12},{15,14},{17,16},{19,... | collective-permute-start | bytes 1572872 | tf_op jit(solution)/shard_map/ppermute | solution.py:144
  24.2 35.6 %collective-permute-start = (bf16[2,4,256,128]{3,2,1,0:T(8,128)(2,1)S(1)}, bf16[2,4,256,128]{3,2,1,0:T(8,128)(2,1)S(1)}, u32[]{:S(2)}, u32[]{:S(2)}) collective-permute-start(bf16[2,4,256,128]{3,2,1,0:T(8,128)(2,1)S(1)} %maximum_bitcast_fusion.kv_ref), channel_id=1, source_target_pairs={{0,2},{1,3},{2,4},{3,5},{4,6},{5,7},{6,8},{7,9},{8,10},{9,11},{10,... | collective-permute-start | bytes 1572872 | tf_op jit(solution)/shard_map/ppermute | solution.py:144
  43.9 0.8 copy-start.4
  59.8 0.8 copy-start.2
  59.8 15.0 %copy-start.5 = (bf16[2,4,256,128]{3,2,1,0:T(8,128)(2,1)S(1)}, bf16[2,4,256,128]{3,2,1,0:T(8,128)(2,1)}, u32[]{:S(2)}) copy-start(bf16[2,4,256,128]{3,2,1,0:T(8,128)(2,1)} %get-tuple-element.22) | copy-start | bytes 1572868
  59.9 18.5 %collective-permute-start.4 = (bf16[2,4,256,128]{3,2,1,0:T(8,128)(2,1)S(1)}, bf16[2,4,256,128]{3,2,1,0:T(8,128)(2,1)S(1)}, u32[]{:S(2)}, u32[]{:S(2)}) collective-permute-start(bf16[2,4,256,128]{3,2,1,0:T(8,128)(2,1)S(1)} %broadcast_select_fusion), channel_id=1, source_target_pairs={{0,1},{1,0},{2,3},{3,2},{4,5},{5,4},{6,7},{7,6},{8,9},{9,8},{10,11... | collective-permute-start | bytes 1572872 | tf_op jit(solution)/shard_map/ppermute | solution.py:144
  70.0 27.3 %collective-permute-start.7 = (bf16[2,4,256,128]{3,2,1,0:T(8,128)(2,1)}, bf16[2,4,256,128]{3,2,1,0:T(8,128)(2,1)S(1)}, u32[]{:S(2)}, u32[]{:S(2)}) collective-permute-start(bf16[2,4,256,128]{3,2,1,0:T(8,128)(2,1)} %get-tuple-element.23), channel_id=1, source_target_pairs={{2,0},{3,1},{4,2},{5,3},{6,4},{7,5},{8,6},{9,7},{10,8},{11,9},{12,... | collective-permute-start | bytes 1572872 | tf_op jit(solution)/shard_map/ppermute | solution.py:144
  71.9 33.6 %collective-permute-start.5 = (bf16[2,4,256,128]{3,2,1,0:T(8,128)(2,1)}, bf16[2,4,256,128]{3,2,1,0:T(8,128)(2,1)S(1)}, u32[]{:S(2)}, u32[]{:S(2)}) collective-permute-start(bf16[2,4,256,128]{3,2,1,0:T(8,128)(2,1)} %get-tuple-element.21), channel_id=1, source_target_pairs={{2,32},{3,33},{4,34},{5,35},{6,36},{7,37},{8,38},{9,39},{10,40},{1... | collective-permute-start | bytes 1572872 | tf_op jit(solution)/shard_map/ppermute | solution.py:144
  74.8 36.5 %collective-permute-start.6 = (bf16[2,4,256,128]{3,2,1,0:T(8,128)(2,1)S(1)}, bf16[2,4,256,128]{3,2,1,0:T(8,128)(2,1)S(1)}, u32[]{:S(2)}, u32[]{:S(2)}) collective-permute-start(bf16[2,4,256,128]{3,2,1,0:T(8,128)(2,1)S(1)} %copy-done.5), channel_id=1, source_target_pairs={{1,32},{2,33},{3,34},{4,35},{5,36},{6,37},{7,38},{8,39},{9,40},{10... | collective-permute-start | bytes 1572872 | tf_op jit(solution)/shard_map/ppermute | solution.py:144
  78.3 0.8 copy-start.6
  79.1 40.9 %copy-start = (f32[2,4,256,128]{3,2,1,0:T(8,128)S(1)}, f32[2,4,256,128]{3,2,1,0:T(8,128)}, u32[]{:S(2)}) copy-start(f32[2,4,256,128]{3,2,1,0:T(8,128)} %get-tuple-element.20) | copy-start | bytes 3145732
  88.6 31.4 %collective-permute-start.8 = (bf16[2,4,256,128]{3,2,1,0:T(8,128)(2,1)}, bf16[2,4,256,128]{3,2,1,0:T(8,128)(2,1)S(1)}, u32[]{:S(2)}, u32[]{:S(2)}) collective-permute-start(bf16[2,4,256,128]{3,2,1,0:T(8,128)(2,1)} %get-tuple-element.24), channel_id=1, source_target_pairs={{1,0},{2,1},{3,2},{4,3},{5,4},{6,5},{7,6},{8,7},{9,8},{10,9},{11,1... | collective-permute-start | bytes 1572872 | tf_op jit(solution)/shard_map/ppermute | solution.py:144

commit v3 on v2

v3 whole, which is shorter than its diff:
```python
import functools
import math

import jax
import jax.numpy as jnp
from jax import lax
from jax.experimental import pallas as pl
from jax.experimental.pallas import tpu as pltpu
from jax.sharding import PartitionSpec as P


LOG2E = math.log2(math.e)
F32, BF16 = jnp.float32, jnp.bfloat16
NT = (((1,), (1,)), ((), ()))
NN = (((1,), (0,)), ((), ()))
TN = (((0,), (0,)), ((), ()))


def mm(a, b, dims):
    return lax.dot_general(a, b, dims, preferred_element_type=F32)


def columns(width, q, g, lse, dot, sl, k, v, mask):
    qc, gc = q[sl, :], g[sl, :]
    s = mm(k, qc, NT)
    p = jnp.exp2(s * (LOG2E * width**-0.5) - lse[:, sl])
    if mask is not None:
        p = jnp.where(mask, p, 0.0)
    dv = mm(p.astype(BF16), gc, NN)
    dp = mm(v, gc, NT)
    ds = (p * (dp - dot[:, sl])).astype(BF16)
    dk = mm(ds, qc, NN)
    dq = mm(ds, k, TN)
    return dq, dk, dv


def own_kernel(cw, step, q_hbm, g_hbm, lse_ref, dot_ref, kv_ref, q_ref, g_ref, dq_ref, out_ref, sems):
    groups, tokens, heads, width = q_ref.shape
    n = tokens * heads

    def copies(j):
        rows = pl.ds(pl.multiple_of(j * heads, heads), heads)
        return [
            pltpu.make_async_copy(src.at[:, rows, :], dst.at[j], sems.at[i, j])
            for i, (src, dst) in enumerate(((q_hbm, q_ref), (g_hbm, g_ref)))
        ]

    for j in range(groups):
        for copy in copies(j):
            copy.start()

    def group(j, carry):
        for copy in copies(j):
            copy.wait()
        q, g = q_ref.at[j].reshape(n, width), g_ref.at[j].reshape(n, width)
        dq_rows = dq_ref.at[j].reshape(n, width)
        parts = []
        for c in range(n // cw):
            sl = pl.ds(c * cw, cw)
            seen = pl.cdiv((c + 1) * cw // heads, step) * step
            k, v = kv_ref[0, j, :seen, :], kv_ref[1, j, :seen, :]
            key = lax.broadcasted_iota(jnp.int32, (seen, cw), 0)
            column = lax.broadcasted_iota(jnp.int32, (seen, cw), 1) + c * cw
            mask = key * heads <= column
            dqc, dkc, dvc = columns(width, q, g, lse_ref.at[j], dot_ref.at[j], sl, k, v, mask)
            dq_rows[sl, :] = dqc
            parts.append((dkc * width**-0.5, dvc))
        done = 0
        for seen in sorted({dk.shape[0] for dk, _ in parts}):
            rows = [(dk[done:seen], dv[done:seen]) for dk, dv in parts if dk.shape[0] >= seen]
            out_ref[0, j, done:seen, :] = sum(dk for dk, _ in rows)
            out_ref[1, j, done:seen, :] = sum(dv for _, dv in rows)
            done = seen
        return carry

    lax.fori_loop(0, groups, group, 0)


def earlier_kernel(cw, merge, last, q_ref, g_ref, lse_ref, dot_ref, prev_ref, *rest):
    n_in = sum(merge)
    in_refs, dq_out, rest = rest[:n_in], rest[n_in], rest[n_in + 1 :]
    outs, scratch = rest[: len(merge)], rest[len(merge) :]
    groups, tokens, heads, width = q_ref.shape
    n = tokens * heads

    def copy_out(j):
        rows = pl.ds(pl.multiple_of(j * heads, heads), heads)
        return pltpu.make_async_copy(scratch[0].at[j], dq_out.at[:, rows, :], scratch[1].at[j])

    def group(j, carry):
        q, g = q_ref.at[j].reshape(n, width), g_ref.at[j].reshape(n, width)
        prev = prev_ref.at[j].reshape(n, width)
        dq_rows = (scratch[0] if last else dq_out).at[j].reshape(n, width)
        blocks, refs = [], in_refs
        for count in merge:
            k, v = refs[0][0, j], refs[0][1, j]
            for other in refs[1:count]:
                k, v = k + other[0, j], v + other[1, j]
            blocks.append((k, v))
            refs = refs[count:]
        k = jnp.concatenate([k for k, _ in blocks], axis=0)
        v = jnp.concatenate([v for _, v in blocks], axis=0)
        dk = dv = None
        for c in range(n // cw):
            sl = pl.ds(c * cw, cw)
            dqc, dkc, dvc = columns(width, q, g, lse_ref.at[j], dot_ref.at[j], sl, k, v, None)
            dqc = dqc + prev[sl, :]
            dq_rows[sl, :] = dqc * width**-0.5 if last else dqc
            dk = dkc if dk is None else dk + dkc
            dv = dvc if dv is None else dv + dvc
        if last:
            copy_out(j).start()
        dk = dk * width**-0.5
        for i, out in enumerate(outs):
            out[0, j] = dk[i * tokens : (i + 1) * tokens].astype(BF16)
            out[1, j] = dv[i * tokens : (i + 1) * tokens].astype(BF16)
        return carry

    lax.fori_loop(0, groups, group, 0)
    if last:
        for j in range(groups):
            copy_out(j).wait()


VMEM = pl.BlockSpec(memory_space=pltpu.VMEM)
HBM = pl.BlockSpec(memory_space=pltpu.HBM)


def in_hbm(x):
    return pltpu.with_memory_space_constraint(x, pltpu.HBM)


def in_vmem(x):
    return pltpu.with_memory_space_constraint(x, pltpu.VMEM)


def work(blocks, rows, tokens, width):
    pairs = blocks * rows * tokens
    return pl.CostEstimate(flops=10 * pairs * width, transcendentals=pairs, bytes_accessed=16 << 20)


def own_call(q, g, lse, dots, kv):
    tokens, heads, width = q.shape
    groups = kv.shape[1]
    shape = (groups, tokens, heads // groups, width)
    return pl.pallas_call(
        functools.partial(own_kernel, 1024, 128),
        in_specs=[HBM, HBM, VMEM, VMEM, VMEM],
        out_specs=[VMEM, VMEM, VMEM, VMEM],
        out_shape=[
            pltpu.VMEM(shape, BF16),
            pltpu.VMEM(shape, BF16),
            pltpu.VMEM(shape, F32),
            jax.ShapeDtypeStruct(kv.shape, F32),
        ],
        scratch_shapes=[pltpu.SemaphoreType.DMA((2, groups))],
        compiler_params=pltpu.CompilerParams(vmem_limit_bytes=LIMIT),
        cost_estimate=work(1, heads * tokens, tokens, width),
        name="own",
    )(in_hbm(q), in_hbm(g), lse, dots, kv)


def earlier_call(q, g, lse, dots, prev, blocks, last):
    groups, tokens, per, width = q.shape
    parts = [part for block in blocks for part in block]
    merge = tuple(len(block) for block in blocks)
    if last:
        dq_shape = jax.ShapeDtypeStruct((tokens, groups * per, width), F32)
        scratch = [pltpu.VMEM(q.shape, F32), pltpu.SemaphoreType.DMA((groups,))]
    else:
        dq_shape, scratch = pltpu.VMEM(q.shape, F32), []
    return pl.pallas_call(
        functools.partial(earlier_kernel, 512 if len(blocks) > 1 else 1024, merge, last),
        in_specs=[VMEM] * (5 + len(parts)),
        out_specs=[HBM if last else VMEM] + [VMEM] * len(blocks),
        out_shape=[dq_shape] + [jax.ShapeDtypeStruct(parts[0].shape, BF16)] * len(blocks),
        scratch_shapes=scratch,
        input_output_aliases={} if last else {4: 0},
        compiler_params=pltpu.CompilerParams(vmem_limit_bytes=LIMIT),
        cost_estimate=work(len(blocks), groups * per * tokens, tokens, width),
    )(in_vmem(q), in_vmem(g), lse, dots, in_vmem(prev), *parts)


LIMIT = 24 << 20


def send(x, by_doc, to):
    docs, ctxs = lax.axis_size("doc"), lax.axis_size("ctx")
    pairs = []
    for d in range(docs):
        for c in range(ctxs):
            t = to(c)
            if t is not None and 0 <= t < ctxs:
                pairs.append((d * ctxs + c, (d + by_doc) % docs * ctxs + t))
    return lax.ppermute(x, ("doc", "ctx"), pairs)


def ahead(c):
    return c + 2


def back_one(c):
    return c - 1


def back_two(c):
    return c - 2


def swap(c):
    return c ^ 1


def even_to_odd(c):
    return c + 1 if c % 2 == 0 else None


def odd_to_even(c):
    return c - 1 if c % 2 == 1 else None


def by_group(x, groups):
    heads, tokens = x.shape
    return x.reshape(groups, heads // groups, tokens).transpose(0, 2, 1).reshape(groups, 1, -1)


def step(queries, stored_key_state, stored_value_state, out_grad, logsumexp, row_dots):
    groups = stored_key_state.shape[2]
    q, g = queries[0], out_grad[0]
    odd = lax.axis_index("ctx") & 1 == 1
    kv = jnp.stack([stored_key_state[0], stored_value_state[0]]).transpose(0, 2, 1, 3)
    kv, odd = lax.optimization_barrier((kv, odd))

    part_far = send(kv, -1, ahead)
    part_near_odd = send(kv, -1, even_to_odd)
    own_far = send(kv, 0, ahead)
    part_near_even = send(part_far, 0, odd_to_even)

    lse = by_group(logsumexp[0] * LOG2E, groups)
    dots = by_group(row_dots[0], groups)
    q, g, dq, own_grad = own_call(q, g, lse, dots, kv)
    dq, grad = earlier_call(q, g, lse, dots, dq, [[part_far]], False)
    part_far_home = send(grad, 1, back_two)
    own_far, dq = lax.optimization_barrier((own_far, dq))
    dq, grad = earlier_call(q, g, lse, dots, dq, [[own_far]], False)
    own_far_home = send(grad, 0, back_two)
    own_near = send(jnp.where(odd, own_far, kv), 0, swap)
    dq, grad = earlier_call(q, g, lse, dots, dq, [[part_near_odd, part_near_even]], False)
    part_near_home = send(grad, 1, back_one)
    dq, grad = earlier_call(q, g, lse, dots, dq, [[own_near]], True)
    own_near_home = send(grad, 0, back_one)

    total = own_grad + part_far_home.astype(F32) + part_near_home.astype(F32)
    total = total + own_far_home.astype(F32) + own_near_home.astype(F32)
    total = total.transpose(0, 2, 1, 3)
    return dq[None], total[0][None], total[1][None]


def solution(mesh):
    rows, vecs = P("doc", "ctx", None, None), P("doc", None, "ctx")
    return jax.shard_map(
        step,
        mesh=mesh,
        in_specs=(rows, rows, rows, rows, vecs, vecs),
        out_specs=(rows, rows, rows),
        check_vma=False,
    )
```

time: 123 us -> 98.7 us (0.80)
  the two profiles are of different devices: /device:TPU:121 before, /device:TPU:183 now
where the time goes in v3:
time: 98.7 us; the launch traced here: 98.3 us
  Pallas kernels  34.5 us (35%)
  waiting for transfers between devices  33.3 us (34%)
  starting transfers between devices  22.5 us (23%)
  local copies, waits for them, and re-layouts  6.04 us (6%)
  other arithmetic  1.16 us (1%)
    ppermute x9, waiting for transfers between devices, send(): return lax.ppermute(x, ('doc', 'ctx'), pairs)  33.3 us
    pallas_call x4, Pallas kernels, earlier_call(): pl.pallas_call(functools.partial(earlier_kernel, 512 if len(blocks) > 1 e...  27.5 us
    ppermute x9, starting transfers between devices, send(): return lax.ppermute(x, ('doc', 'ctx'), pairs)  22.5 us
    pallas_call x1, Pallas kernels, own_call(): pl.pallas_call(functools.partial(own_kernel, 1024, 128), in_specs=[HBM, H...  7.01 us
    unnamed x4, local copies, waits for them, and re-layouts  4.24 us
  transfers between devices with their start and end apart: 9, of which 6 were waited for; matrix products, arithmetic and copies ran while one was open for 3% of the time, Pallas kernels for 35%

profile of v3, /device:TPU:183, one launch (start us, length us, event | category | flops | bytes accessed | tf_op | source)
XLA Modules:
  0.0 98.3 jit_solution(288195785581989532)
XLA Ops:
  0.6 1.0 %copy.20 = bf16[1,256,4,128]{3,1,2,0:T(8,128)(2,1)S(1)} copy(bf16[1,256,4,128]{3,2,1,0:T(4,128)(2,1)} %param.7) | data formatting | bytes 524288 | tf_op args[1]
  1.6 1.0 %copy.21 = bf16[1,256,4,128]{3,1,2,0:T(8,128)(2,1)S(1)} copy(bf16[1,256,4,128]{3,2,1,0:T(4,128)(2,1)} %param.8) | data formatting | bytes 524288 | tf_op args[2]
  2.7 2.7 %collective-permute-start.1 = (bf16[2,4,256,128]{3,2,1,0:T(8,128)(2,1)S(1)}, bf16[2,4,256,128]{3,2,1,0:T(8,128)(2,1)S(1)}, u32[]{:S(2)}, u32[]{:S(2)}) collective-permute-start(bf16[2,4,256,128]{3,2,1,0:T(8,128)(2,1)S(1)} %maximum_bitcast_fusion.kv_ref), channel_id=1, source_target_pairs={{0,226},{1,227},{2,228},{3,229},{4,230},{5,231},{6,232},{7,233},{8... | collective-permute-start | bytes 1572872 | tf_op jit(solution)/shard_map/ppermute | solution.py:195
  5.4 1.3 %collective-permute-start.2 = (bf16[2,4,256,128]{3,2,1,0:T(8,128)(2,1)S(1)}, bf16[2,4,256,128]{3,2,1,0:T(8,128)(2,1)S(1)}, u32[]{:S(2)}, u32[]{:S(2)}) collective-permute-start(bf16[2,4,256,128]{3,2,1,0:T(8,128)(2,1)S(1)} %maximum_bitcast_fusion.kv_ref), channel_id=1, source_target_pairs={{0,225},{2,227},{4,229},{6,231},{8,233},{10,235},{12,237},{14,239}... | collective-permute-start | bytes 1572872 | tf_op jit(solution)/shard_map/ppermute | solution.py:195
  6.7 4.8 %collective-permute-start = (bf16[2,4,256,128]{3,2,1,0:T(8,128)(2,1)S(1)}, bf16[2,4,256,128]{3,2,1,0:T(8,128)(2,1)S(1)}, u32[]{:S(2)}, u32[]{:S(2)}) collective-permute-start(bf16[2,4,256,128]{3,2,1,0:T(8,128)(2,1)S(1)} %maximum_bitcast_fusion.kv_ref), channel_id=1, source_target_pairs={{0,2},{1,3},{2,4},{3,5},{4,6},{5,7},{6,8},{7,9},{8,10},{9,11},{10,... | collective-permute-start | bytes 1572872 | tf_op jit(solution)/shard_map/ppermute | solution.py:195
  11.5 0.8 multiply_bitcast_fusion
  12.3 0.2 copy.18
  12.5 0.3 reshape.18.lse_ref
  12.8 1.0 copy.19
  13.7 0.3 reshape.19.dot_ref
  14.0 7.0 %own.1 = (bf16[4,256,8,128]{3,2,1,0:T(8,128)(2,1)S(1)}, bf16[4,256,8,128]{3,2,1,0:T(8,128)(2,1)S(1)}, f32[4,256,8,128]{3,2,1,0:T(8,128)S(1)}, f32[2,4,256,128]{3,2,1,0:T(8,128)S(1)}) custom-call(bf16[256,32,128]{2,1,0:T(8,128)(2,1)} %bitcast.15, bf16[256,32,128]{2,1,0:T(8,128)(2,1)} %bitcast.16, f32[4,1,2048]{2,1,0:T(1,128)S(1)} %reshape.18.lse_ref, ...), custom_call_target="tpu_custom_call" | custom-call | flops 2684354560 | bytes 16777216 | tf_op jit(solution)/shard_map/own/pallas_call | solution.py:146
  21.1 2.8 %collective-permute-done.1.rest_0_ = bf16[2,4,256,128]{3,2,1,0:T(8,128)(2,1)S(1)} collective-permute-done((bf16[2,4,256,128]{3,2,1,0:T(8,128)(2,1)S(1)}, bf16[2,4,256,128]{3,2,1,0:T(8,128)(2,1)S(1)}, u32[]{:S(2)}, u32[]{:S(2)}) %collective-permute-start.1) | collective-permute-done | bytes 524320 | tf_op jit(solution)/shard_map/ppermute | solution.py:195
  23.9 6.7 %shard_map.85 = (f32[4,256,8,128]{3,2,1,0:T(8,128)S(1)}, bf16[2,4,256,128]{3,2,1,0:T(8,128)(2,1)S(1)}) custom-call(bf16[4,256,8,128]{3,2,1,0:T(8,128)(2,1)S(1)} %get-tuple-element.20.q_ref, bf16[4,256,8,128]{3,2,1,0:T(8,128)(2,1)S(1)} %get-tuple-element.21.g_ref, f32[4,1,2048]{2,1,0:T(1,128)S(1)} %reshape.18.lse_ref, ...), custom_call_target="tpu_custom_call", output_to_operand_aliasing={{0}: (4, {})} | custom-call | flops 2684354560 | bytes 16777216 | tf_op jit(solution)/shard_map/pallas_call | solution.py:172
  30.6 5.0 %collective-permute-done.rest_0_ = bf16[2,4,256,128]{3,2,1,0:T(8,128)(2,1)S(1)} collective-permute-done((bf16[2,4,256,128]{3,2,1,0:T(8,128)(2,1)S(1)}, bf16[2,4,256,128]{3,2,1,0:T(8,128)(2,1)S(1)}, u32[]{:S(2)}, u32[]{:S(2)}) %collective-permute-start) | collective-permute-done | bytes 524320 | tf_op jit(solution)/shard_map/ppermute | solution.py:195
  35.5 3.7 %collective-permute-start.3 = (bf16[2,4,256,128]{3,2,1,0:T(8,128)(2,1)S(1)}, bf16[2,4,256,128]{3,2,1,0:T(8,128)(2,1)S(1)}, u32[]{:S(2)}, u32[]{:S(2)}) collective-permute-start(bf16[2,4,256,128]{3,2,1,0:T(8,128)(2,1)S(1)} %collective-permute-done.1.rest_0_), channel_id=1, source_target_pairs={{1,0},{3,2},{5,4},{7,6},{9,8},{11,10},{13,12},{15,14},{17,16},{19,... | collective-permute-start | bytes 1572872 | tf_op jit(solution)/shard_map/ppermute | solution.py:195
  39.2 0.1 broadcast_select_fusion
  39.3 0.1 collective-permute-start.4
  39.4 6.7 %shard_map.86 = (f32[4,256,8,128]{3,2,1,0:T(8,128)S(1)}, bf16[2,4,256,128]{3,2,1,0:T(8,128)(2,1)S(1)}) custom-call(bf16[4,256,8,128]{3,2,1,0:T(8,128)(2,1)S(1)} %get-tuple-element.20.q_ref, bf16[4,256,8,128]{3,2,1,0:T(8,128)(2,1)S(1)} %get-tuple-element.21.g_ref, f32[4,1,2048]{2,1,0:T(1,128)S(1)} %reshape.18.lse_ref, ...), custom_call_target="tpu_custom_call", output_to_operand_aliasing={{0}: (4, {})} | custom-call | flops 2684354560 | bytes 16777216 | tf_op jit(solution)/shard_map/pallas_call | solution.py:172
  46.1 2.9 %collective-permute-start.7 = (bf16[2,4,256,128]{3,2,1,0:T(8,128)(2,1)S(1)}, bf16[2,4,256,128]{3,2,1,0:T(8,128)(2,1)S(1)}, u32[]{:S(2)}, u32[]{:S(2)}) collective-permute-start(bf16[2,4,256,128]{3,2,1,0:T(8,128)(2,1)S(1)} %get-tuple-element.33), channel_id=1, source_target_pairs={{2,0},{3,1},{4,2},{5,3},{6,4},{7,5},{8,6},{9,7},{10,8},{11,9},{12,... | collective-permute-start | bytes 1572872 | tf_op jit(solution)/shard_map/ppermute | solution.py:195
  49.1 1.9 %collective-permute-start.5 = (bf16[2,4,256,128]{3,2,1,0:T(8,128)(2,1)S(1)}, bf16[2,4,256,128]{3,2,1,0:T(8,128)(2,1)S(1)}, u32[]{:S(2)}, u32[]{:S(2)}) collective-permute-start(bf16[2,4,256,128]{3,2,1,0:T(8,128)(2,1)S(1)} %get-tuple-element.31), channel_id=1, source_target_pairs={{2,32},{3,33},{4,34},{5,35},{6,36},{7,37},{8,38},{9,39},{10,40},{1... | collective-permute-start | bytes 1572872 | tf_op jit(solution)/shard_map/ppermute | solution.py:195
  51.0 6.7 %shard_map.87 = (f32[4,256,8,128]{3,2,1,0:T(8,128)S(1)}, bf16[2,4,256,128]{3,2,1,0:T(8,128)(2,1)S(1)}) custom-call(bf16[4,256,8,128]{3,2,1,0:T(8,128)(2,1)S(1)} %get-tuple-element.20.q_ref, bf16[4,256,8,128]{3,2,1,0:T(8,128)(2,1)S(1)} %get-tuple-element.21.g_ref, f32[4,1,2048]{2,1,0:T(1,128)S(1)} %reshape.18.lse_ref, ...), custom_call_target="tpu_custom_call", output_to_operand_aliasing={{0}: (4, {})} | custom-call | flops 2684354560 | bytes 16777216 | tf_op jit(solution)/shard_map/pallas_call | solution.py:172
  57.7 2.3 %collective-permute-start.6 = (bf16[2,4,256,128]{3,2,1,0:T(8,128)(2,1)S(1)}, bf16[2,4,256,128]{3,2,1,0:T(8,128)(2,1)S(1)}, u32[]{:S(2)}, u32[]{:S(2)}) collective-permute-start(bf16[2,4,256,128]{3,2,1,0:T(8,128)(2,1)S(1)} %get-tuple-element.32), channel_id=1, source_target_pairs={{1,32},{2,33},{3,34},{4,35},{5,36},{6,37},{7,38},{8,39},{9,40},{10... | collective-permute-start | bytes 1572872 | tf_op jit(solution)/shard_map/ppermute | solution.py:195
  60.0 7.4 %shard_map.88 = (f32[256,32,128]{2,1,0:T(8,128)}, bf16[2,4,256,128]{3,2,1,0:T(8,128)(2,1)S(1)}) custom-call(bf16[4,256,8,128]{3,2,1,0:T(8,128)(2,1)S(1)} %get-tuple-element.20.q_ref, bf16[4,256,8,128]{3,2,1,0:T(8,128)(2,1)S(1)} %get-tuple-element.21.g_ref, f32[4,1,2048]{2,1,0:T(1,128)S(1)} %reshape.18.lse_ref, f32[4,1,2048]{2,1,0:T(1,128)S(1)} %reshape.19.dot_ref, ...), custom_call_target="tpu_custom_call" | custom-call | flops 2684354560 | bytes 16777216 | tf_op jit(solution)/shard_map/pallas_call | solution.py:172
  67.4 2.7 %collective-permute-start.8 = (bf16[2,4,256,128]{3,2,1,0:T(8,128)(2,1)S(1)}, bf16[2,4,256,128]{3,2,1,0:T(8,128)(2,1)S(1)}, u32[]{:S(2)}, u32[]{:S(2)}) collective-permute-start(bf16[2,4,256,128]{3,2,1,0:T(8,128)(2,1)S(1)} %get-tuple-element.34), channel_id=1, source_target_pairs={{1,0},{2,1},{3,2},{4,3},{5,4},{6,5},{7,6},{8,7},{9,8},{10,9},{11,1... | collective-permute-start | bytes 1572872 | tf_op jit(solution)/shard_map/ppermute | solution.py:195
  70.2 4.3 %collective-permute-done.7 = bf16[2,4,256,128]{3,2,1,0:T(8,128)(2,1)S(1)} collective-permute-done((bf16[2,4,256,128]{3,2,1,0:T(8,128)(2,1)S(1)}, bf16[2,4,256,128]{3,2,1,0:T(8,128)(2,1)S(1)}, u32[]{:S(2)}, u32[]{:S(2)}) %collective-permute-start.7) | collective-permute-done | bytes 524320 | tf_op jit(solution)/shard_map/ppermute | solution.py:195
  74.4 0.1 collective-permute-done.5
  74.5 6.4 %collective-permute-done.6 = bf16[2,4,256,128]{3,2,1,0:T(8,128)(2,1)S(1)} collective-permute-done((bf16[2,4,256,128]{3,2,1,0:T(8,128)(2,1)S(1)}, bf16[2,4,256,128]{3,2,1,0:T(8,128)(2,1)S(1)}, u32[]{:S(2)}, u32[]{:S(2)}) %collective-permute-start.6) | collective-permute-done | bytes 524320 | tf_op jit(solution)/shard_map/ppermute | solution.py:195
  80.9 14.7 %collective-permute-done.8 = bf16[2,4,256,128]{3,2,1,0:T(8,128)(2,1)S(1)} collective-permute-done((bf16[2,4,256,128]{3,2,1,0:T(8,128)(2,1)S(1)}, bf16[2,4,256,128]{3,2,1,0:T(8,128)(2,1)S(1)}, u32[]{:S(2)}, u32[]{:S(2)}) %collective-permute-start.8) | collective-permute-done | bytes 524320 | tf_op jit(solution)/shard_map/ppermute | solution.py:195
  95.6 0.3 add_bitcast_fusion
  95.9 0.1 fusion
  96.0 1.1 %copy.33 = f32[1,256,4,128]{3,2,1,0:T(4,128)} copy(f32[1,256,4,128]{3,1,2,0:T(8,128)S(1)} %get-tuple-element.41) | data formatting | bytes 1048576
  97.1 1.1 %copy.32 = f32[1,256,4,128]{3,2,1,0:T(4,128)} copy(f32[1,256,4,128]{3,1,2,0:T(8,128)S(1)} %get-tuple-element.42) | data formatting | bytes 1048576
  (4 shorter events, 0.1 us)
Async XLA Ops:
  2.7 21.2 %collective-permute-start.1 = (bf16[2,4,256,128]{3,2,1,0:T(8,128)(2,1)S(1)}, bf16[2,4,256,128]{3,2,1,0:T(8,128)(2,1)S(1)}, u32[]{:S(2)}, u32[]{:S(2)}) collective-permute-start(bf16[2,4,256,128]{3,2,1,0:T(8,128)(2,1)S(1)} %maximum_bitcast_fusion.kv_ref), channel_id=1, source_target_pairs={{0,226},{1,227},{2,228},{3,229},{4,230},{5,231},{6,232},{7,233},{8... | collective-permute-start | bytes 1572872 | tf_op jit(solution)/shard_map/ppermute | solution.py:195
  5.4 45.6 %collective-permute-start.2 = (bf16[2,4,256,128]{3,2,1,0:T(8,128)(2,1)S(1)}, bf16[2,4,256,128]{3,2,1,0:T(8,128)(2,1)S(1)}, u32[]{:S(2)}, u32[]{:S(2)}) collective-permute-start(bf16[2,4,256,128]{3,2,1,0:T(8,128)(2,1)S(1)} %maximum_bitcast_fusion.kv_ref), channel_id=1, source_target_pairs={{0,225},{2,227},{4,229},{6,231},{8,233},{10,235},{12,237},{14,239}... | collective-permute-start | bytes 1572872 | tf_op jit(solution)/shard_map/ppermute | solution.py:195
  6.7 28.9 %collective-permute-start = (bf16[2,4,256,128]{3,2,1,0:T(8,128)(2,1)S(1)}, bf16[2,4,256,128]{3,2,1,0:T(8,128)(2,1)S(1)}, u32[]{:S(2)}, u32[]{:S(2)}) collective-permute-start(bf16[2,4,256,128]{3,2,1,0:T(8,128)(2,1)S(1)} %maximum_bitcast_fusion.kv_ref), channel_id=1, source_target_pairs={{0,2},{1,3},{2,4},{3,5},{4,6},{5,7},{6,8},{7,9},{8,10},{9,11},{10,... | collective-permute-start | bytes 1572872 | tf_op jit(solution)/shard_map/ppermute | solution.py:195
  35.5 15.5 %collective-permute-start.3 = (bf16[2,4,256,128]{3,2,1,0:T(8,128)(2,1)S(1)}, bf16[2,4,256,128]{3,2,1,0:T(8,128)(2,1)S(1)}, u32[]{:S(2)}, u32[]{:S(2)}) collective-permute-start(bf16[2,4,256,128]{3,2,1,0:T(8,128)(2,1)S(1)} %collective-permute-done.1.rest_0_), channel_id=1, source_target_pairs={{1,0},{3,2},{5,4},{7,6},{9,8},{11,10},{13,12},{15,14},{17,16},{19,... | collective-permute-start | bytes 1572872 | tf_op jit(solution)/shard_map/ppermute | solution.py:195
  39.3 20.7 %collective-permute-start.4 = (bf16[2,4,256,128]{3,2,1,0:T(8,128)(2,1)S(1)}, bf16[2,4,256,128]{3,2,1,0:T(8,128)(2,1)S(1)}, u32[]{:S(2)}, u32[]{:S(2)}) collective-permute-start(bf16[2,4,256,128]{3,2,1,0:T(8,128)(2,1)S(1)} %broadcast_select_fusion), channel_id=1, source_target_pairs={{0,1},{1,0},{2,3},{3,2},{4,5},{5,4},{6,7},{7,6},{8,9},{9,8},{10,11... | collective-permute-start | bytes 1572872 | tf_op jit(solution)/shard_map/ppermute | solution.py:195
  46.1 28.3 %collective-permute-start.7 = (bf16[2,4,256,128]{3,2,1,0:T(8,128)(2,1)S(1)}, bf16[2,4,256,128]{3,2,1,0:T(8,128)(2,1)S(1)}, u32[]{:S(2)}, u32[]{:S(2)}) collective-permute-start(bf16[2,4,256,128]{3,2,1,0:T(8,128)(2,1)S(1)} %get-tuple-element.33), channel_id=1, source_target_pairs={{2,0},{3,1},{4,2},{5,3},{6,4},{7,5},{8,6},{9,7},{10,8},{11,9},{12,... | collective-permute-start | bytes 1572872 | tf_op jit(solution)/shard_map/ppermute | solution.py:195
  49.1 25.5 %collective-permute-start.5 = (bf16[2,4,256,128]{3,2,1,0:T(8,128)(2,1)S(1)}, bf16[2,4,256,128]{3,2,1,0:T(8,128)(2,1)S(1)}, u32[]{:S(2)}, u32[]{:S(2)}) collective-permute-start(bf16[2,4,256,128]{3,2,1,0:T(8,128)(2,1)S(1)} %get-tuple-element.31), channel_id=1, source_target_pairs={{2,32},{3,33},{4,34},{5,35},{6,36},{7,37},{8,38},{9,39},{10,40},{1... | collective-permute-start | bytes 1572872 | tf_op jit(solution)/shard_map/ppermute | solution.py:195
  57.7 23.2 %collective-permute-start.6 = (bf16[2,4,256,128]{3,2,1,0:T(8,128)(2,1)S(1)}, bf16[2,4,256,128]{3,2,1,0:T(8,128)(2,1)S(1)}, u32[]{:S(2)}, u32[]{:S(2)}) collective-permute-start(bf16[2,4,256,128]{3,2,1,0:T(8,128)(2,1)S(1)} %get-tuple-element.32), channel_id=1, source_target_pairs={{1,32},{2,33},{3,34},{4,35},{5,36},{6,37},{7,38},{8,39},{9,40},{10... | collective-permute-start | bytes 1572872 | tf_op jit(solution)/shard_map/ppermute | solution.py:195
  67.4 28.2 %collective-permute-start.8 = (bf16[2,4,256,128]{3,2,1,0:T(8,128)(2,1)S(1)}, bf16[2,4,256,128]{3,2,1,0:T(8,128)(2,1)S(1)}, u32[]{:S(2)}, u32[]{:S(2)}) collective-permute-start(bf16[2,4,256,128]{3,2,1,0:T(8,128)(2,1)S(1)} %get-tuple-element.34), channel_id=1, source_target_pairs={{1,0},{2,1},{3,2},{4,3},{5,4},{6,5},{7,6},{8,7},{9,8},{10,9},{11,1... | collective-permute-start | bytes 1572872 | tf_op jit(solution)/shard_map/ppermute | solution.py:195
